TPU v7x, 128 devices: a whole 4x4x4 slice. The times are simulated.
128 devices in a mesh: row: 8 (over y, x_lo), col: 16 (over x_hi, z, core).
Axes of the slice: x: 4 (x_hi: 2, x_lo: 2; x = x_hi * 2 + x_lo), y: 4, z: 4, core: 2. Of those that a mesh axis runs over, the one named last changes fastest.
Arguments:
- patches: bfloat16 [64, 128, 768], P('row', 'col'), may hold values from -6 to 6
- w_patch: bfloat16 [768, 6144], replicated, may hold values from -0.21875 to 0.21875
- patch_bias: bfloat16 [6144], replicated, may hold values from -5 to 5
- ln_gain: bfloat16 [6144], replicated, may hold values from 0.5 to 1.5
- w_qkv: bfloat16 [6144, 3, 48, 128], P(None, None, 'col'), may hold values from -1 to 1
- qk_gain: float32 [2, 48, 128], P(None, 'col'), may hold values from 0 to 6, as said below
- w_out: bfloat16 [48, 128, 6144], P('col', None, 'row'), may hold values from -0.078125 to 0.078125
Outputs:
- attn_branch: bfloat16 [8192, 6144], P(('row', 'col'))
Inputs may be any that keep to these rules, and one draw needn't show every extreme that they name: `qk_gain`: positive gains.
All inputs are finite; a program needn't handle non-finite values.
Results may differ from a plain program's by a relative error of at most 0.015.
Values may be sent and summed in bfloat16 or wider, within the bound.
A program may use at most 320 MiB of HBM per device.

v0:
```python
import math

import jax
import jax.numpy as jnp
from jax import lax
from jax.sharding import PartitionSpec as P

NORM_EPS = 1e-06


def sincos_table(row_ids, col_ids, model_width):
    quarter = model_width // 4
    frequency = 1.0 / 10000.0 ** (jnp.arange(quarter, dtype=jnp.float32) / quarter)
    row_angle = row_ids.astype(jnp.float32)[:, None] * frequency[None, :]
    col_angle = col_ids.astype(jnp.float32)[:, None] * frequency[None, :]
    return jnp.concatenate(
        [jnp.sin(row_angle), jnp.cos(row_angle), jnp.sin(col_angle), jnp.cos(col_angle)], axis=1
    )


def layer_norm(values, gain_row):
    mean_val = jnp.mean(values, axis=-1, keepdims=True)
    centered = values - mean_val
    variance = jnp.mean(centered * centered, axis=-1, keepdims=True)
    return centered * lax.rsqrt(variance + NORM_EPS) * gain_row


def local(patches, w_patch, patch_bias, ln_gain, w_qkv, qk_gain, w_out):
    tile_rows, tile_cols, pixel_width = patches.shape
    model_width = w_patch.shape[1]
    heads_here = w_qkv.shape[2]
    head_size = w_qkv.shape[3]
    col_count = lax.axis_size("col")
    block_tokens = tile_rows * tile_cols * col_count
    row_anchor = lax.axis_index("row") * tile_rows
    qkv_matrix = w_qkv.reshape(model_width, 3 * heads_here * head_size)
    bias_row = patch_bias.astype(jnp.float32)[None, :]
    gain_row = ln_gain.astype(jnp.float32)
    piece_cols = patches.shape[1]
    local_rows = jnp.repeat(jnp.arange(tile_rows, dtype=jnp.int32), piece_cols)
    local_cols = jnp.tile(jnp.arange(piece_cols, dtype=jnp.int32), tile_rows)
    flat_pixels = patches.reshape(tile_rows * piece_cols, pixel_width)
    embedded = jnp.dot(flat_pixels, w_patch, preferred_element_type=jnp.float32) + bias_row
    embedded = embedded + sincos_table(
        row_anchor + local_rows, lax.axis_index("col") * tile_cols + local_cols, model_width
    )
    normed = layer_norm(embedded, gain_row).astype(jnp.bfloat16)
    own_tile = normed.reshape(tile_rows, piece_cols, model_width)
    normed_piece = lax.all_gather(own_tile, "col", axis=1, tiled=True)
    piece_cols = normed_piece.shape[1]
    flat_normed = normed_piece.reshape(tile_rows * piece_cols, model_width)
    projected = jnp.dot(flat_normed, qkv_matrix, preferred_element_type=jnp.float32)
    projected = projected.reshape(tile_rows, piece_cols, 3 * heads_here * head_size)
    projected = projected.reshape(block_tokens, 3, heads_here, head_size)
    queries = layer_norm(projected[:, 0], qk_gain[0]).astype(jnp.bfloat16)
    keys_here = layer_norm(projected[:, 1], qk_gain[1]).astype(jnp.bfloat16)
    values_here = projected[:, 2].astype(jnp.bfloat16)
    query_heads = queries.transpose(1, 0, 2)
    scale_factor = 1.0 / math.sqrt(head_size)
    start_state = (
        jnp.full((heads_here, block_tokens), -1e30, jnp.float32),
        jnp.zeros((heads_here, block_tokens), jnp.float32),
        jnp.zeros((heads_here, block_tokens, head_size), jnp.float32),
    )
    key_piece = lax.all_gather(keys_here, "row", axis=0, tiled=True)
    value_piece = lax.all_gather(values_here, "row", axis=0, tiled=True)
    piece_len = key_piece.shape[0]
    key_block = math.gcd(piece_len, 1024)
    block_count = piece_len // key_block
    key_blocks = key_piece.reshape(block_count, key_block, heads_here, head_size)
    value_blocks = value_piece.reshape(block_count, key_block, heads_here, head_size)

    def step_block(state, block_args):
        run_peak, run_total, run_acc = state
        block_keys, block_values = block_args
        scores = (
            jnp.einsum("hqd,khd->hqk", query_heads, block_keys, preferred_element_type=jnp.float32)
            * scale_factor
        )
        new_peak = jnp.maximum(run_peak, jnp.max(scores, axis=2))
        rescale = jnp.exp(run_peak - new_peak)
        exponent = jnp.exp(scores - new_peak[:, :, None])
        new_total = run_total * rescale + jnp.sum(exponent, axis=2)
        weighted = jnp.einsum(
            "hqk,khd->hqd",
            exponent.astype(jnp.bfloat16),
            block_values,
            preferred_element_type=jnp.float32,
        )
        new_acc = run_acc * rescale[:, :, None] + weighted
        return ((new_peak, new_total, new_acc), None)

    final_state, unused = lax.scan(step_block, start_state, (key_blocks, value_blocks))
    peak_all, total_all, acc_all = final_state
    context = (acc_all / total_all[:, :, None]).astype(jnp.bfloat16)
    context = context.transpose(1, 0, 2).reshape(block_tokens, heads_here * head_size)
    out_weight = lax.all_gather(w_out, "row", axis=2, tiled=True).reshape(
        heads_here * head_size, model_width
    )
    return lax.psum_scatter(
        jnp.dot(context, out_weight, preferred_element_type=jnp.float32).astype(jnp.bfloat16),
        "col",
        scatter_dimension=0,
        tiled=True,
    )


def solution(mesh):
    return jax.shard_map(
        local,
        mesh=mesh,
        in_specs=(
            P("row", "col", None),
            P(),
            P(),
            P(),
            P(None, None, "col", None),
            P(None, "col", None),
            P("col", None, "row"),
        ),
        out_specs=P(("row", "col"), None),
        check_vma=False,
    )
```

profile of v0, /device:TPU:25, one launch (start us, length us, event | category | flops | bytes accessed | tf_op | source)
XLA Modules:
  0.0 725.3 jit_solution(8967606610263915652)
XLA Ops:
  6.6 0.1 convert_element_type.50
  6.7 0.1 convert_element_type.52
  6.7 0.7 convert_element_type.48
  7.5 2.8 multiply_sine_fusion.1
  10.3 5.6 fusion.27
  15.8 0.3 multiply_reduce_fusion.2
  16.2 0.3 copy-done.4
  16.5 1.1 fusion.22
  17.7 0.0 all-gather.8.cloned.1.call-start
  17.8 18.8 %copy.13 = bf16[6144,3,3,128]{0,3,2,1:T(8,128)(2,1)} copy(bf16[6144,3,3,128]{3,0,2,1:T(8,128)(2,1)} %param.13) | data formatting | bytes 28311552 | tf_op args[4]
  36.6 74.4 %all-gather.6.cloned.1.call-done = bf16[8,128,6144]{2,1,0:T(8,128)(2,1)} async-done(((bf16[8,8,6144]{2,1,0:T(8,128)(2,1)}), bf16[8,128,6144]{2,1,0:T(8,128)(2,1)}) %all-gather.6.cloned.1.call-update) | async-done | bytes 12582928 | tf_op jit(solution)/shard_map/all_gather | solution.py:49
  111.0 19.3 %fusion.19 = f32[1024,3,3,128]{0,3,2,1:T(8,128)S(1)} fusion(bf16[1024,6144,1,1]{1,0,3,2:T(8,128)(2,1)} %bitcast.97, bf16[6144,3,3,128]{0,3,2,1:T(8,128)(2,1)} %copy.13), kind=kOutput, calls=%fused_computation.23 | convolution fusion | flops 14495514624 | bytes 31457280 | tf_op jit(solution)/shard_map/dot_general | solution.py:52
  130.3 0.3 slice_reduce_fusion
  130.6 0.4 multiply_reduce_fusion
  131.1 1.3 copy-done.3
  132.4 1.4 fusion.23
  133.8 0.0 all-gather.12.cloned.1.call-start
  133.8 2.4 slice.33
  136.2 0.0 all-gather.12.cloned.1.call-update
  136.2 0.0 all-gather.10.cloned.1.call-start
  136.3 0.5 all-gather.10.cloned.1.call-update
  136.8 0.2 reduce-scatter.2.cloned.1.call-start
  137.1 1.2 copy.15
  138.2 121.7 %all-gather.8.cloned.1.call-done = bf16[8192,3,128]{0,2,1:T(8,128)(2,1)} async-done(((bf16[1024,3,128]{0,2,1:T(8,128)(2,1)}), bf16[8192,3,128]{0,2,1:T(8,128)(2,1)}) %all-gather.8.cloned.1.call-update) | async-done | bytes 6291472 | tf_op jit(solution)/shard_map/all_gather | solution.py:65
  259.9 12.7 %copy.21 = bf16[48,8,8,1024]{3,2,1,0:T(8,128)(2,1)} copy(bf16[48,8,8,1024]{3,1,2,0:T(8,128)(2,1)} %bitcast.95) | data formatting | bytes 12582912
  272.6 9.1 %copy.14 = bf16[8,1024,3,128]{3,1,2,0:T(8,128)(2,1)} copy(bf16[8,1024,3,128]{1,0,3,2:T(8,128)(2,1)} %bitcast.93) | data formatting | bytes 12582912
  281.8 109.8 %all-gather.12.cloned.1.call-done = bf16[8192,1,3,128]{0,3,2,1:T(8,128)(2,1)} async-done(((bf16[1024,1,3,128]{0,3,2,1:T(8,128)(2,1)}), bf16[8192,1,3,128]{0,3,2,1:T(8,128)(2,1)}) %all-gather.12.cloned.1.call-update) | async-done | bytes 6291472 | tf_op jit(solution)/shard_map/all_gather | solution.py:66
  391.6 12.7 %copy.22 = bf16[48,8,8,1024]{3,2,1,0:T(8,128)(2,1)} copy(bf16[48,8,8,1024]{3,1,2,0:T(8,128)(2,1)} %bitcast.96) | data formatting | bytes 12582912
  404.3 9.2 %copy.16 = bf16[8,1024,3,128]{3,1,2,0:T(8,128)(2,1)} copy(bf16[8,1024,3,128]{1,0,3,2:T(8,128)(2,1)} %bitcast.94) | data formatting | bytes 12582912
  413.5 170.3 %while.15 = (s32[]{:T(128)}, f32[3,1024]{1,0:T(4,128)S(1)}, f32[3,1024]{1,0:T(4,128)S(1)}, f32[3,1024,128]{2,1,0:T(8,128)}, bf16[8,1024,3,128]{3,1,2,0:T(8,128)(...) while((s32[]{:T(128)}, f32[3,1024]{1,0:T(4,128)S(1)}, ...), condition=%wide.region_9.10_spmd.clone, body=%wide.region_6.9_spmd.clone.sunk | while | flops 1636973568 | bytes 93783168 | solution.py:93
  413.5 7.8 %bitcast_reduce_fusion.2 = (f32[3,1024]{1,0:T(4,128)S(1)}, f32[3,1024,1024]{2,1,0:T(8,128)}) fusion(bf16[3,1024,128]{2,1,0:T(8,128)(2,1)} %get-tuple-element.195, bf16[8,1024,3,128]{3,1,2,0:T(8,128)(2,1)} %get-tuple-element.194, s32[]{:T(128)} %get-tuple-element.181), kind=kOutput, calls=%fused_computation.1.clone.1 | convolution fusion | flops 811594752 | bytes 14168576 | tf_op jit(solution)/shard_map/while/body/eval_jaxpr/hqd,khd->hqk/dot_general | solution.py:77
  421.3 6.8 fusion.41
  428.2 1.4 copy-done.2
  429.6 5.1 fusion.43
  434.7 7.7 %bitcast_reduce_fusion.2 = (f32[3,1024]{1,0:T(4,128)S(1)}, f32[3,1024,1024]{2,1,0:T(8,128)}) fusion(bf16[3,1024,128]{2,1,0:T(8,128)(2,1)} %get-tuple-element.195, bf16[8,1024,3,128]{3,1,2,0:T(8,128)(2,1)} %get-tuple-element.194, s32[]{:T(128)} %get-tuple-element.181), kind=kOutput, calls=%fused_computation.1.clone.1 | convolution fusion | flops 811594752 | bytes 14168576 | tf_op jit(solution)/shard_map/while/body/eval_jaxpr/hqd,khd->hqk/dot_general | solution.py:77
  442.4 6.8 fusion.41
  449.3 1.4 copy-done.2
  450.7 5.4 fusion.43
  456.1 7.8 %bitcast_reduce_fusion.2 = (f32[3,1024]{1,0:T(4,128)S(1)}, f32[3,1024,1024]{2,1,0:T(8,128)}) fusion(bf16[3,1024,128]{2,1,0:T(8,128)(2,1)} %get-tuple-element.195, bf16[8,1024,3,128]{3,1,2,0:T(8,128)(2,1)} %get-tuple-element.194, s32[]{:T(128)} %get-tuple-element.181), kind=kOutput, calls=%fused_computation.1.clone.1 | convolution fusion | flops 811594752 | bytes 14168576 | tf_op jit(solution)/shard_map/while/body/eval_jaxpr/hqd,khd->hqk/dot_general | solution.py:77
  463.8 6.8 fusion.41
  470.7 1.4 copy-done.2
  472.1 5.4 fusion.43
  477.5 7.8 %bitcast_reduce_fusion.2 = (f32[3,1024]{1,0:T(4,128)S(1)}, f32[3,1024,1024]{2,1,0:T(8,128)}) fusion(bf16[3,1024,128]{2,1,0:T(8,128)(2,1)} %get-tuple-element.195, bf16[8,1024,3,128]{3,1,2,0:T(8,128)(2,1)} %get-tuple-element.194, s32[]{:T(128)} %get-tuple-element.181), kind=kOutput, calls=%fused_computation.1.clone.1 | convolution fusion | flops 811594752 | bytes 14168576 | tf_op jit(solution)/shard_map/while/body/eval_jaxpr/hqd,khd->hqk/dot_general | solution.py:77
  485.2 6.8 fusion.41
  492.1 1.3 copy-done.2
  493.4 5.4 fusion.43
  498.8 7.7 %bitcast_reduce_fusion.2 = (f32[3,1024]{1,0:T(4,128)S(1)}, f32[3,1024,1024]{2,1,0:T(8,128)}) fusion(bf16[3,1024,128]{2,1,0:T(8,128)(2,1)} %get-tuple-element.195, bf16[8,1024,3,128]{3,1,2,0:T(8,128)(2,1)} %get-tuple-element.194, s32[]{:T(128)} %get-tuple-element.181), kind=kOutput, calls=%fused_computation.1.clone.1 | convolution fusion | flops 811594752 | bytes 14168576 | tf_op jit(solution)/shard_map/while/body/eval_jaxpr/hqd,khd->hqk/dot_general | solution.py:77
  506.5 6.8 fusion.41
  513.3 1.3 copy-done.2
  514.7 5.4 fusion.43
  520.0 7.7 %bitcast_reduce_fusion.2 = (f32[3,1024]{1,0:T(4,128)S(1)}, f32[3,1024,1024]{2,1,0:T(8,128)}) fusion(bf16[3,1024,128]{2,1,0:T(8,128)(2,1)} %get-tuple-element.195, bf16[8,1024,3,128]{3,1,2,0:T(8,128)(2,1)} %get-tuple-element.194, s32[]{:T(128)} %get-tuple-element.181), kind=kOutput, calls=%fused_computation.1.clone.1 | convolution fusion | flops 811594752 | bytes 14168576 | tf_op jit(solution)/shard_map/while/body/eval_jaxpr/hqd,khd->hqk/dot_general | solution.py:77
  527.8 6.8 fusion.41
  534.6 1.3 copy-done.2
  535.9 5.4 fusion.43
  541.3 7.7 %bitcast_reduce_fusion.2 = (f32[3,1024]{1,0:T(4,128)S(1)}, f32[3,1024,1024]{2,1,0:T(8,128)}) fusion(bf16[3,1024,128]{2,1,0:T(8,128)(2,1)} %get-tuple-element.195, bf16[8,1024,3,128]{3,1,2,0:T(8,128)(2,1)} %get-tuple-element.194, s32[]{:T(128)} %get-tuple-element.181), kind=kOutput, calls=%fused_computation.1.clone.1 | convolution fusion | flops 811594752 | bytes 14168576 | tf_op jit(solution)/shard_map/while/body/eval_jaxpr/hqd,khd->hqk/dot_general | solution.py:77
  549.1 6.8 fusion.41
  555.9 1.3 copy-done.2
  557.2 5.4 fusion.43
  562.6 7.7 %bitcast_reduce_fusion.2 = (f32[3,1024]{1,0:T(4,128)S(1)}, f32[3,1024,1024]{2,1,0:T(8,128)}) fusion(bf16[3,1024,128]{2,1,0:T(8,128)(2,1)} %get-tuple-element.195, bf16[8,1024,3,128]{3,1,2,0:T(8,128)(2,1)} %get-tuple-element.194, s32[]{:T(128)} %get-tuple-element.181), kind=kOutput, calls=%fused_computation.1.clone.1 | convolution fusion | flops 811594752 | bytes 14168576 | tf_op jit(solution)/shard_map/while/body/eval_jaxpr/hqd,khd->hqk/dot_general | solution.py:77
  570.3 6.8 fusion.41
  577.2 1.3 copy-done.2
  578.5 5.4 fusion.43
  583.9 11.9 %bitcast_convert_fusion = bf16[1024,6144]{1,0:T(8,128)(2,1)} fusion(bf16[3,128,6144]{2,1,0:T(8,128)(2,1)} %all-gather.10.cloned.1.call-done, f32[3,1024,128]{2,1,0:T(8,128)} %get-tuple-element.43, f32[3,1024]{1,0:T(4,128)S(1)} %get-tuple-element.44), kind=kOutput, calls=%fused_computation.22 | convolution fusion | flops 4838916096 | bytes 18886656 | tf_op jit(solution)/shard_map/dot_general | solution.py:101
  595.8 123.0 %reduce-scatter.2.cloned.1.call-done = bf16[64,6144]{1,0:T(8,128)(2,1)} async-done(((bf16[1024,6144]{1,0:T(8,128)(2,1)}), bf16[64,6144]{1,0:T(8,128)(2,1)}) %reduce-scatter.2.cloned.1.call-update) | async-done | bytes 786448 | tf_op jit(solution)/shard_map/reduce_scatter | solution.py:100
  (59 shorter events, 0.5 us)
Async XLA Ops:
  6.5 3.7 copy-start
  6.5 104.4 %all-gather.6.cloned.1.call-start = ((), (), s32[]{:S(2)}) async-start(), calls=%async_computation.1 | async-start | bytes 13369344 | tf_op jit(solution)/shard_map/all_gather | solution.py:49
  15.8 0.7 copy-start.4
  17.7 18.9 %copy-start.5 = (f32[2,3,128]{2,0,1:T(2,128)S(1)}, f32[2,3,128]{2,0,1:T(2,128)}, u32[]{:S(2)}) copy-start(f32[2,3,128]{2,0,1:T(2,128)} %param.14) | copy-start | bytes 9220
  17.7 242.2 %all-gather.8.cloned.1.call-start = ((), (), s32[]{:S(2)}) async-start(), calls=%async_computation.2 | async-start | bytes 7077888 | tf_op jit(solution)/shard_map/all_gather | solution.py:65
  130.3 2.1 copy-start.3
  133.8 257.8 %all-gather.12.cloned.1.call-start = ((), (), s32[]{:S(2)}) async-start(), calls=%async_computation.5 | async-start | bytes 7077888 | tf_op jit(solution)/shard_map/all_gather | solution.py:66
  136.2 447.6 %all-gather.10.cloned.1.call-start = ((), (), s32[]{:S(2)}) async-start(), calls=%async_computation.3 | async-start | bytes 5308416 | tf_op jit(solution)/shard_map/all_gather | solution.py:97
  136.8 581.9 %reduce-scatter.2.cloned.1.call-start = ((), (), s32[]{:S(2)}) async-start(), calls=%async_computation.4 | async-start | bytes 13369344 | tf_op jit(solution)/shard_map/reduce_scatter | solution.py:100
  421.3 8.3 %copy-start.2 = (f32[3,1024,1024]{2,1,0:T(8,128)S(1)}, f32[3,1024,1024]{2,1,0:T(8,128)}, u32[]{:S(2)}) copy-start(f32[3,1024,1024]{2,1,0:T(8,128)} %get-tuple-element.169) | copy-start | bytes 37748740 | tf_op jit(solution)/shard_map/while
  442.4 8.3 %copy-start.2 = (f32[3,1024,1024]{2,1,0:T(8,128)S(1)}, f32[3,1024,1024]{2,1,0:T(8,128)}, u32[]{:S(2)}) copy-start(f32[3,1024,1024]{2,1,0:T(8,128)} %get-tuple-element.169) | copy-start | bytes 37748740 | tf_op jit(solution)/shard_map/while
  463.8 8.3 %copy-start.2 = (f32[3,1024,1024]{2,1,0:T(8,128)S(1)}, f32[3,1024,1024]{2,1,0:T(8,128)}, u32[]{:S(2)}) copy-start(f32[3,1024,1024]{2,1,0:T(8,128)} %get-tuple-element.169) | copy-start | bytes 37748740 | tf_op jit(solution)/shard_map/while
  485.2 8.2 %copy-start.2 = (f32[3,1024,1024]{2,1,0:T(8,128)S(1)}, f32[3,1024,1024]{2,1,0:T(8,128)}, u32[]{:S(2)}) copy-start(f32[3,1024,1024]{2,1,0:T(8,128)} %get-tuple-element.169) | copy-start | bytes 37748740 | tf_op jit(solution)/shard_map/while
  506.5 8.2 %copy-start.2 = (f32[3,1024,1024]{2,1,0:T(8,128)S(1)}, f32[3,1024,1024]{2,1,0:T(8,128)}, u32[]{:S(2)}) copy-start(f32[3,1024,1024]{2,1,0:T(8,128)} %get-tuple-element.169) | copy-start | bytes 37748740 | tf_op jit(solution)/shard_map/while
  527.8 8.2 %copy-start.2 = (f32[3,1024,1024]{2,1,0:T(8,128)S(1)}, f32[3,1024,1024]{2,1,0:T(8,128)}, u32[]{:S(2)}) copy-start(f32[3,1024,1024]{2,1,0:T(8,128)} %get-tuple-element.169) | copy-start | bytes 37748740 | tf_op jit(solution)/shard_map/while
  549.1 8.2 %copy-start.2 = (f32[3,1024,1024]{2,1,0:T(8,128)S(1)}, f32[3,1024,1024]{2,1,0:T(8,128)}, u32[]{:S(2)}) copy-start(f32[3,1024,1024]{2,1,0:T(8,128)} %get-tuple-element.169) | copy-start | bytes 37748740 | tf_op jit(solution)/shard_map/while
  570.3 8.2 %copy-start.2 = (f32[3,1024,1024]{2,1,0:T(8,128)S(1)}, f32[3,1024,1024]{2,1,0:T(8,128)}, u32[]{:S(2)}) copy-start(f32[3,1024,1024]{2,1,0:T(8,128)} %get-tuple-element.169) | copy-start | bytes 37748740 | tf_op jit(solution)/shard_map/while
  595.8 123.0 %copy-start.1 = (bf16[8,8,768]{2,1,0:T(8,128)(2,1)S(1)}, bf16[8,8,768]{2,1,0:T(8,128)(2,1)}, u32[]{:S(2)}) copy-start(bf16[8,8,768]{2,1,0:T(8,128)(2,1)} %param.9) | copy-start | bytes 294916
Sparse Core Ops, SparseCore 0:
  17.8 93.1 all-gather.5
  133.9 126.0 all-gather.7
  261.6 129.9 all-gather.11
  393.1 100.4 all-gather.9
  595.9 122.8 reduce-scatter.1
where the time goes:
time: 728 us; the launch traced here: 725 us
  waiting for transfers between devices  429 us (59%)
  matrix products  141 us (19%)
  local copies, waits for them, and re-layouts  78.8 us (11%)
  other arithmetic  61.9 us (9%)
  between operations  13.3 us (2%)
    reduce_scatter x1, waiting for transfers between devices, local(): lax.psum_scatter(jnp.dot(context, out_weight, preferred_element_type=jnp....  123 us
    all_gather x1, waiting for transfers between devices, local(): key_piece = lax.all_gather(keys_here, 'row', axis=0, tiled=True)  122 us
    all_gather x1, waiting for transfers between devices, local(): value_piece = lax.all_gather(values_here, 'row', axis=0, tiled=True)  110 us
    all_gather x1, waiting for transfers between devices, local(): normed_piece = lax.all_gather(own_tile, 'col', axis=1, tiled=True)  74.4 us
    unnamed x17, local copies, waits for them, and re-layouts  65.4 us
    dot_general x8, matrix products, step_block(): jnp.einsum('hqd,khd->hqk', query_heads, block_keys, preferred_element_typ...  62 us
    reduce_sum x8, other arithmetic, step_block(): new_total = run_total * rescale + jnp.sum(exponent, axis=2)  54.5 us
    dot_general x8, matrix products, step_block(): jnp.einsum('hqk,khd->hqd', exponent.astype(jnp.bfloat16), block_values, p...  42.6 us
  transfers between devices with their start and end apart: 5, of which 4 were waited for; matrix products, arithmetic and copies ran while one was open for 31% of the time, Pallas kernels for 0%

commit v1 on v0

v1 whole, which is shorter than its diff:
```python
import functools
import math

import numpy as np
import jax
import jax.numpy as jnp
from jax import lax
from jax.experimental import pallas as pl
from jax.experimental.pallas import tpu as pltpu
from jax.sharding import PartitionSpec as P

NORM_EPS = 1e-06
MESH = pl.DeviceIdType.MESH
F32 = jnp.float32
BF16 = jnp.bfloat16
ORDERS = ((0, 1, 2), (1, 2, 0), (2, 0, 1))
LHS_ROWS = 992
ROW_C, ROW_R, ROW_BIAS, ROW_GAIN = 768, 896, 960, 961
VMEM_LIMIT = 67043328


def place():
    r = lax.axis_index("row")
    m = lax.axis_index("col")
    x = (m // 8) * 2 + r % 2
    y = r // 2
    z = (m // 2) % 4
    c = m % 2
    return x, y, z, c


def device(x, y, z, c):
    return (y * 2 + x % 2, (x // 2) * 8 + z * 2 + c)


def trig_tables():
    quarter = 1536
    freq = 10000.0 ** (-np.arange(quarter, dtype=np.float64) / quarter)
    coarse = 8.0 * np.arange(16, dtype=np.float64)[:, None] * freq[None, :]
    fine = np.arange(8, dtype=np.float64)[:, None] * freq[None, :]
    f = lambda a: a.astype(np.float32)
    return f(np.sin(coarse)), f(np.cos(coarse)), f(np.sin(fine)), f(np.cos(fine))


def prep_kernel(
    pown, p2d, bias_ref, gain_ref, sa, ca, sb, cb, wp_hbm, wq_hbm,
    buf, rsbuf, wout, rpos, cpos,
    wp, lhs, wq, emb, res, mu, rsown,
    ssem, rsem, pss, prs, xss, xrs, lsem, wsem, osem,
):
    x, y, z, c = place()
    coord = (x, y, z)
    row = lax.axis_index("row")
    col = lax.axis_index("col")

    def near(axis, d):
        t = list(coord)
        t[axis] = (t[axis] + d) % 4
        return device(t[0], t[1], t[2], c)

    partner = device(x, y, z, 1 - c)

    def piece(p, ph, val, core, half=None):
        order = ORDERS[p]
        idx = []
        for b in range(3):
            if b in order[:ph]:
                idx.append(pl.ds(0, 4))
            elif b == order[ph]:
                idx.append(val)
            else:
                idx.append(coord[b])
        tail = () if half is None else (half,)
        if half is None:
            return buf.at[(p, *idx, core)]
        return buf.at[(p, *idx, core, half)]

    def ring(p, ph, slot, recv):
        axis = ORDERS[p][ph]
        own = coord[axis]
        if slot < 2:
            if recv:
                src = piece(p, ph, (own + (3 if slot == 0 else 1)) % 4, c)
                dst = src
            else:
                dst = piece(p, ph, own, c)
                src = pown.at[p] if ph == 0 else dst
        else:
            if recv:
                src = piece(p, ph, (own + 2) % 4, c, slot - 2)
            else:
                src = piece(p, ph, (own + (3 if slot == 2 else 1)) % 4, c, slot - 2)
            dst = src
        to = near(axis, 1 if slot % 2 == 0 else 3)
        return pltpu.make_async_remote_copy(
            src_ref=src, dst_ref=dst, send_sem=ssem.at[p, ph, slot], recv_sem=rsem.at[p, ph, slot],
            device_id=to, device_id_type=MESH)

    def across(p, k, recv):
        core = 1 - c if recv else c
        own = coord[ORDERS[p][2]]
        val = (own, (own + 3) % 4, (own + 1) % 4, (own + 2) % 4, (own + 2) % 4)[k]
        ref = piece(p, 2, val, core, None if k < 3 else k - 3)
        return pltpu.make_async_remote_copy(
            src_ref=ref, dst_ref=ref, send_sem=pss.at[p, k], recv_sem=prs.at[p, k],
            device_id=partner, device_id_type=MESH)

    def rs_copy(step, d, recv):
        if step == 0:
            core = 1 - c if recv else c
            dst = rsbuf.at[x, y, z, core]
            src = dst if recv else rsown
            to = partner
        else:
            axis = step - 1
            idx = []
            for b in range(3):
                if b < axis:
                    idx.append(pl.ds(0, 4))
                elif b == axis:
                    idx.append((coord[b] + 4 - d) % 4 if recv else coord[b])
                else:
                    idx.append(coord[b])
            dst = rsbuf.at[tuple(idx)]
            src = dst
            to = near(axis, d)
        return pltpu.make_async_remote_copy(
            src_ref=src, dst_ref=dst, send_sem=xss.at[step, d], recv_sem=xrs.at[step, d],
            device_id=to, device_id_type=MESH)

    def start_phase(ph):
        for slot in (0, 1):
            for p in range(3):
                ring(p, ph, slot, False).start()

    def forward_phase(ph):
        for slot in (0, 1):
            for p in range(3):
                ring(p, ph, slot, True).wait_recv()
                ring(p, ph, slot + 2, False).start()
                if ph == 2:
                    across(p, 1 + slot, False).start()

    def finish_phase(ph):
        for slot in (2, 3):
            for p in range(3):
                ring(p, ph, slot, True).wait_recv()
                if ph == 2:
                    across(p, 1 + slot, False).start()

    def rs_step(step):
        for d in ((0,) if step == 0 else (1, 2, 3)):
            rs_copy(step, d, False).start()

    def rs_wait(step):
        for d in ((0,) if step == 0 else (1, 2, 3)):
            rs_copy(step, d, True).wait_recv()

    wp_copies = [pltpu.make_async_copy(wp_hbm.at[pl.ds(i * 192, 192)], wp.at[pl.ds(i * 192, 192)], lsem.at[i]) for i in range(4)]
    for cp in wp_copies:
        cp.start()
    wq_copies = [pltpu.make_async_copy(wq_hbm.at[b // 3, b % 3], wq.at[b], wsem.at[b]) for b in range(9)]
    for cp in wq_copies:
        cp.start()

    barrier = pltpu.get_barrier_semaphore()
    peers = [near(a, d) for a in range(3) for d in (1, 2, 3)] + [partner]
    for peer in peers:
        pl.semaphore_signal(barrier, inc=1, device_id=peer, device_id_type=MESH)
    pl.semaphore_wait(barrier, len(peers))

    start_phase(0)
    own_copy = pltpu.make_async_copy(pown, buf.at[pl.ds(0, 3), x, y, z, c], osem.at[0])
    own_copy.start()

    gain = gain_ref[...]
    gain_lo, gain_hi = gain[:, :3072], gain[:, 3072:]
    bias = bias_ref[...]

    lhs[ROW_C:ROW_C + 128, 0:3072] = jnp.zeros((128, 3072), BF16)
    lhs[ROW_R:ROW_R + 64, 3072:6144] = jnp.zeros((64, 3072), BF16)
    sbv, cbv = sb[...], cb[...]
    for t in range(8):
        sins, coss = [], []
        for u in (2 * t, 2 * t + 1):
            sav, cav = sa[u:u + 1, :], ca[u:u + 1, :]
            sins.append(sav * cbv + cav * sbv)
            coss.append(cav * cbv - sav * sbv)
        table = jnp.concatenate([jnp.concatenate(sins, 0), jnp.concatenate(coss, 0)], axis=1)
        mu[16 * t:16 * t + 16, :] = jnp.broadcast_to(jnp.sum(table, axis=1, keepdims=True) * (1.0 / 6144), (16, 128))
        lhs[ROW_C + 16 * t:ROW_C + 16 * t + 16, 3072:6144] = (table * gain_hi).astype(BF16)
        if t < 4:
            lhs[ROW_R + 16 * t:ROW_R + 16 * t + 16, 0:3072] = (table * gain_lo).astype(BF16)
    bias_c = (bias - jnp.mean(bias, axis=1, keepdims=True)) * gain
    tail_rows = lax.broadcasted_iota(jnp.int32, (32, 6144), 0)
    lhs[ROW_BIAS:ROW_BIAS + 32, :] = jnp.where(
        tail_rows == 0, bias_c, jnp.where(tail_rows == 1, gain, 0.0)).astype(BF16)

    for cp in wp_copies:
        cp.wait()
    forward_phase(0)

    def own_table(n):
        sav, cav = sa[pl.ds(n, 1), :], ca[pl.ds(n, 1), :]
        return jnp.concatenate([sav * cbv + cav * sbv, cav * cbv - sav * sbv], axis=1)

    t_row, t_col = own_table(row), own_table(col)
    pixels = p2d[...]
    total = jnp.zeros((64, 1), F32)
    for n in range(12):
        lo = n * 512
        e = jnp.dot(pixels, wp[:, lo:lo + 512], preferred_element_type=F32) + bias[:, lo:lo + 512]
        e = e.reshape(8, 8, 512)
        if n < 6:
            e = e + t_row[:, lo:lo + 512].reshape(8, 1, 512)
        else:
            e = e + t_col[:, lo - 3072:lo - 2560].reshape(1, 8, 512)
        e = e.reshape(64, 512)
        emb[:, lo:lo + 512] = e
        total = total + jnp.sum(e, axis=1, keepdims=True)
    mean = total * (1.0 / 6144)
    square = jnp.zeros((64, 1), F32)
    for n in range(12):
        d = emb[:, n * 512:n * 512 + 512] - mean
        square = square + jnp.sum(d * d, axis=1, keepdims=True)
    rstd = lax.rsqrt(square * (1.0 / 6144) + NORM_EPS)
    rs_wide = jnp.concatenate([jnp.broadcast_to(rstd, (64, 128)), jnp.zeros((64, 128), F32)], axis=0)
    rsown[...] = rs_wide.T[0:1, :]

    finish_phase(0)
    own_copy.wait()
    start_phase(1)
    rs_own_copy = pltpu.make_async_copy(rsown, rsbuf.at[x, y, z, c], osem.at[1])
    rs_own_copy.start()
    rs_step(0)

    def center(i, carry):
        w = wp[pl.ds(pl.multiple_of(i * 48, 48), 48), :].astype(F32)
        w = (w - jnp.mean(w, axis=1, keepdims=True)) * gain
        lhs[pl.ds(pl.multiple_of(i * 48, 48), 48), :] = w.astype(BF16)
        return carry

    lax.fori_loop(0, 8, center, 0)
    forward_phase(1)
    rs_own_copy.wait()
    rs_wait(0)
    rs_step(1)
    lax.fori_loop(8, 16, center, 0)
    finish_phase(1)
    start_phase(2)
    for p in range(3):
        across(p, 0, False).start()
    rs_wait(1)
    rs_step(2)
    for cp in wq_copies:
        cp.wait()

    def product(it, carry):
        pair = it // 2
        mt = it % 2
        rows = pl.ds(pl.multiple_of(mt * 496, 496), 496)
        second = jnp.minimum(2 * pair + 1, 8)
        w = jnp.concatenate([wq[2 * pair], wq[second]], axis=1)
        res[pair, rows, :] = jnp.dot(lhs[rows, :], w, preferred_element_type=F32)

        @pl.when(it == 2)
        def _():
            rs_wait(2)
            rs_step(3)

        @pl.when(it == 8)
        def _():
            forward_phase(2)
        return carry

    lax.fori_loop(0, 10, product, 0)

    mus = mu[...]
    for b in range(9):
        lanes = slice((b % 2) * 128, (b % 2) * 128 + 128)
        w = res[b // 2, 0:768, lanes]
        gsum = res[b // 2, ROW_GAIN:ROW_GAIN + 1, lanes]
        rp = res[b // 2, ROW_R:ROW_R + 64, lanes] - mus[:64] * gsum + res[b // 2, ROW_BIAS:ROW_BIAS + 1, lanes]
        cp = res[b // 2, ROW_C:ROW_C + 128, lanes] - mus * gsum
        if b < 6:
            w = w - jnp.mean(w, axis=1, keepdims=True)
            rp = rp - jnp.mean(rp, axis=1, keepdims=True)
            cp = cp - jnp.mean(cp, axis=1, keepdims=True)
        out = slice(b * 128, b * 128 + 128)
        wout[:, out] = w.astype(BF16)
        rpos[:, out] = rp
        cpos[:, out] = cp

    finish_phase(2)
    rs_wait(3)
    for p in range(3):
        for k in range(5):
            across(p, k, True).wait_recv()
    for p in range(3):
        for ph in range(3):
            for slot in range(4):
                ring(p, ph, slot, False).wait_send()
        for k in range(5):
            across(p, k, False).wait_send()
    for step in range(4):
        for d in ((0,) if step == 0 else (1, 2, 3)):
            rs_copy(step, d, False).wait_send()


def prep(pown, p2d, bias, gain, w_patch, w_qkv):
    tables = [jnp.asarray(t) for t in trig_tables()]
    vm = pl.BlockSpec(memory_space=pltpu.VMEM)
    anym = pl.BlockSpec(memory_space=pl.ANY)
    dma = pltpu.SemaphoreType.DMA
    return pl.pallas_call(
        prep_kernel,
        out_shape=(
            jax.ShapeDtypeStruct((3, 4, 4, 4, 2, 2, 32, 256), BF16),
            jax.ShapeDtypeStruct((4, 4, 4, 2, 1, 128), F32),
            jax.ShapeDtypeStruct((768, 1152), BF16),
            jax.ShapeDtypeStruct((64, 1152), F32),
            jax.ShapeDtypeStruct((128, 1152), F32),
        ),
        in_specs=[vm] * 8 + [anym] * 2,
        out_specs=(anym, vm, vm, vm, vm),
        scratch_shapes=[
            pltpu.VMEM((768, 6144), BF16),
            pltpu.VMEM((LHS_ROWS, 6144), BF16),
            pltpu.VMEM((9, 6144, 128), BF16),
            pltpu.VMEM((64, 6144), F32),
            pltpu.VMEM((5, LHS_ROWS, 256), F32),
            pltpu.VMEM((128, 128), F32),
            pltpu.VMEM((1, 128), F32),
            dma((3, 3, 4)), dma((3, 3, 4)), dma((3, 5)), dma((3, 5)),
            dma((4, 4)), dma((4, 4)), dma((4,)), dma((9,)), dma((2,)),
        ],
        compiler_params=pltpu.CompilerParams(collective_id=0, has_side_effects=True, vmem_limit_bytes=VMEM_LIMIT),
        name="prep",
    )(pown, p2d, bias, gain, *tables, w_patch, w_qkv)


def attend_kernel(
    buf, rs_ref, w_ref, rpos, cpos, qk_gain, wo_hbm,
    ctx, wslab,
    tiles, kall, vall, qall, acc, peak,
    tsem, ssem, rsem,
):
    x, y, z, c = place()
    row = lax.axis_index("row")
    x_hi = x // 2

    barrier = pltpu.get_barrier_semaphore()
    slab_to = [device(x_hi * 2 + t % 2, t // 2, row // 2, row % 2) for t in range(8)]
    slab_from = [device(x_hi * 2 + c, z, t // 2, t % 2) for t in range(8)]
    me_target = (row // 2 == z) & (row % 2 == c)
    slot_here = z * 2 + c

    for t in range(8):
        is_self = me_target & (row == t)

        @pl.when(jnp.logical_not(is_self))
        def _():
            pl.semaphore_signal(barrier, inc=1, device_id=slab_to[t], device_id_type=MESH)
        from_self = me_target & (slot_here == t)

        @pl.when(jnp.logical_not(from_self))
        def _():
            pl.semaphore_signal(barrier, inc=1, device_id=slab_from[t], device_id_type=MESH)
    pl.semaphore_wait(barrier, jnp.where(me_target, 14, 16))

    def slab_copy(t):
        return pltpu.make_async_remote_copy(
            src_ref=wo_hbm, dst_ref=wslab.at[slot_here], send_sem=ssem.at[t], recv_sem=rsem.at[slot_here],
            device_id=slab_to[t], device_id_type=MESH)

    def slab_arrival(t):
        return pltpu.make_async_remote_copy(
            src_ref=wo_hbm, dst_ref=wslab.at[t], send_sem=ssem.at[t], recv_sem=rsem.at[t],
            device_id=slab_from[t], device_id_type=MESH)

    def slab_local():
        return pltpu.make_async_copy(wo_hbm, wslab.at[slot_here], rsem.at[slot_here])

    for t in range(8):
        is_self = me_target & (row == t)

        @pl.when(is_self)
        def _():
            slab_local().start()

        @pl.when(jnp.logical_not(is_self))
        def _():
            slab_copy(t).start()

    def tile_copies(n, slot):
        cx, cy, ch = n // 8, (n // 2) % 4, n % 2
        return [
            pltpu.make_async_copy(buf.at[p, cx, cy, pl.ds(ch * 2, 2)], tiles.at[slot, p], tsem.at[slot, p])
            for p in range(3)
        ]

    scale = math.log2(math.e) / math.sqrt(128.0)

    def project(n, slot, first, width):
        cx, cy, ch = n // 8, (n // 2) % 4, n % 2
        p = jnp.concatenate([tiles[slot, q].reshape(256, 256) for q in range(3)], axis=1)
        yv = jnp.dot(p, w_ref[:, first:first + width], preferred_element_type=F32).reshape(4, 8, 8, width)
        r = cy * 2 + cx % 2
        base = (cx // 2) * 64 + ch * 32
        rp = rpos[pl.ds(pl.multiple_of(r * 8, 8), 8), first:first + width]
        cp = cpos[pl.ds(pl.multiple_of(base, 32), 32), first:first + width]
        yv = yv + rp.reshape(1, 8, 1, width) + cp.reshape(4, 1, 8, width)
        rs8 = rs_ref[cx, cy].reshape(8, 128)
        rst = jnp.concatenate([rs8] + [jnp.zeros((120, 128), F32)], axis=0).T
        rst = jnp.where(ch == 0, rst[0:64, 0:4], rst[0:64, 4:8])
        rcol = jnp.concatenate([rst[:, q:q + 1] for q in range(4)], axis=0)
        return yv.reshape(256, width), rcol

    def normed(yh, rcol, gain):
        var = jnp.mean(yh * yh, axis=1, keepdims=True)
        return yh * (rcol * lax.rsqrt(rcol * rcol * var + NORM_EPS)) * gain

    order_count = 32
    for cp in tile_copies(0, 0):
        cp.start()

    def fill(n, carry):
        slot = n % 2

        @pl.when(n + 1 < order_count)
        def _():
            for cp in tile_copies(n + 1, 1 - slot):
                cp.start()
        for cp in tile_copies(n, slot):
            cp.wait()
        cx, cy, ch = n // 8, (n // 2) % 4, n % 2
        yv, rcol = project(n, slot, 384, 768)
        at = pl.ds(pl.multiple_of(n * 256, 256), 256)
        for h in range(3):
            kall[h, at, :] = normed(yv[:, h * 128:h * 128 + 128], rcol, qk_gain[1, h:h + 1, :]).astype(BF16)
            vall[h, at, :] = (yv[:, 384 + h * 128:512 + h * 128] * rcol).astype(BF16)

        @pl.when((cy == y) & (cx % 2 == x % 2))
        def _():
            yq, rq = project(n, slot, 0, 384)
            for h in range(3):
                qh = normed(yq[:, h * 128:h * 128 + 128], rq, qk_gain[0, h:h + 1, :] * scale)
                qh = qh.reshape(4, 8, 8, 128)
                for i in range(8):
                    dst = i * 128 + (cx // 2) * 64 + ch * 32
                    qall[h, pl.ds(pl.multiple_of(dst, 32), 32), :] = qh[:, i].reshape(32, 128).astype(BF16)
        return carry

    lax.fori_loop(0, order_count, fill, 0)

    QT, BK, NCH = 256, 1024, 4
    ones = jnp.ones((BK, 128), BF16)

    def head(h, carry):
        for t in range(NCH):
            acc[t] = jnp.zeros((QT, 256), F32)
            peak[t] = jnp.full((QT, 128), -1e30, F32)

        def block(j, carry2):
            at = pl.ds(pl.multiple_of(j * BK, BK), BK)
            k = kall[h, at, :]
            va = jnp.concatenate([vall[h, at, :], ones], axis=1)
            scores = [
                lax.dot_general(qall[h, t * QT:t * QT + QT, :], k, (((1,), (1,)), ((), ())), preferred_element_type=F32)
                for t in range(NCH)
            ]
            for t in range(NCH):
                old = peak[t][:, :1]
                new = jnp.maximum(old, jnp.max(scores[t], axis=1, keepdims=True))
                p = jnp.exp2(scores[t] - new).astype(BF16)
                acc[t] = acc[t] * jnp.exp2(old - new) + jnp.dot(p, va, preferred_element_type=F32)
                peak[t] = jnp.broadcast_to(new, (QT, 128))
            return carry2

        lax.fori_loop(0, 8192 // BK, block, 0)
        for t in range(NCH):
            a = acc[t]
            ctx[h, t * QT:t * QT + QT, :] = (a[:, :128] / a[:, 128:]).astype(BF16)
        return carry

    lax.fori_loop(0, 3, head, 0)

    for t in range(8):
        from_self = me_target & (slot_here == t)

        @pl.when(from_self)
        def _():
            slab_local().wait()

        @pl.when(jnp.logical_not(from_self))
        def _():
            slab_arrival(t).wait_recv()
        is_self = me_target & (row == t)

        @pl.when(jnp.logical_not(is_self))
        def _():
            slab_copy(t).wait_send()


def attend(buf, rs, w, rpos, cpos, qk_gain, wo):
    vm = pl.BlockSpec(memory_space=pltpu.VMEM)
    anym = pl.BlockSpec(memory_space=pl.ANY)
    dma = pltpu.SemaphoreType.DMA
    return pl.pallas_call(
        attend_kernel,
        out_shape=(
            jax.ShapeDtypeStruct((3, 1024, 128), BF16),
            jax.ShapeDtypeStruct((8, 384, 768), BF16),
        ),
        in_specs=[anym] + [vm] * 5 + [anym],
        out_specs=(vm, anym),
        scratch_shapes=[
            pltpu.VMEM((2, 3, 2, 2, 2, 32, 256), BF16),
            pltpu.VMEM((3, 8192, 128), BF16),
            pltpu.VMEM((3, 8192, 128), BF16),
            pltpu.VMEM((3, 1024, 128), BF16),
            pltpu.VMEM((4, 256, 256), F32),
            pltpu.VMEM((4, 256, 128), F32),
            dma((2, 3)), dma((8,)), dma((8,)),
        ],
        compiler_params=pltpu.CompilerParams(collective_id=1, has_side_effects=True, vmem_limit_bytes=VMEM_LIMIT),
        name="attend",
    )(buf, rs, w, rpos, cpos, qk_gain, wo)


def finish_kernel(ctx, wslab_hbm, out, cbuf, wv, part, rbuf, ssem, rsem, pss, prs, fss, frs, lsem, osem):
    x, y, z, c = place()
    x_hi = x // 2
    row = lax.axis_index("row")
    partner = device(x, y, z, 1 - c)
    wcopy = pltpu.make_async_copy(wslab_hbm, wv, lsem.at[0])
    wcopy.start()

    def core_at(dz):
        return device(x, y, (z + dz) % 4, c)

    def owner(t):
        return (row, t)

    col = lax.axis_index("col")
    barrier = pltpu.get_barrier_semaphore()
    for t in range(16):
        @pl.when(col != t)
        def _():
            pl.semaphore_signal(barrier, inc=1, device_id=owner(t), device_id_type=MESH)
    pl.semaphore_wait(barrier, 15)

    own_copy = pltpu.make_async_copy(ctx, cbuf.at[z, c], osem.at[0])
    own_copy.start()

    def ring(slot, recv):
        if slot < 2:
            if recv:
                src = cbuf.at[(z + (3 if slot == 0 else 1)) % 4, c]
                dst = src
            else:
                src, dst = ctx, cbuf.at[z, c]
        else:
            off = 2 if recv else (3 if slot == 2 else 1)
            src = cbuf.at[(z + off) % 4, c, pl.ds(0, 3), pl.ds((slot - 2) * 512, 512)]
            dst = src
        return pltpu.make_async_remote_copy(
            src_ref=src, dst_ref=dst, send_sem=ssem.at[slot], recv_sem=rsem.at[slot],
            device_id=core_at(1 if slot % 2 == 0 else 3), device_id_type=MESH)

    def across(k, recv):
        core = 1 - c if recv else c
        if k < 3:
            ref = cbuf.at[(z + (0, 3, 1)[k]) % 4, core]
        else:
            ref = cbuf.at[(z + 2) % 4, core, pl.ds(0, 3), pl.ds((k - 3) * 512, 512)]
        src = ctx if (k == 0 and not recv) else ref
        return pltpu.make_async_remote_copy(
            src_ref=src, dst_ref=ref, send_sem=pss.at[k], recv_sem=prs.at[k],
            device_id=partner, device_id_type=MESH)

    ring(0, False).start()
    ring(1, False).start()
    across(0, False).start()
    for slot in (0, 1):
        ring(slot, True).wait_recv()
        ring(slot + 2, False).start()
        across(1 + slot, False).start()
    for slot in (2, 3):
        ring(slot, True).wait_recv()
        across(1 + slot, False).start()
    own_copy.wait()
    wcopy.wait()
    for k in range(5):
        across(k, True).wait_recv()

    slab = z * 2 + c

    def send(t):
        return pltpu.make_async_remote_copy(
            src_ref=part.at[t], dst_ref=rbuf.at[x_hi, slab], send_sem=fss.at[t], recv_sem=frs.at[x_hi, slab],
            device_id=owner(t), device_id_type=MESH)

    def keep(t):
        return pltpu.make_async_copy(part.at[t], rbuf.at[x_hi, slab], osem.at[1])

    def arrival(hi, t):
        return pltpu.make_async_remote_copy(
            src_ref=part.at[0], dst_ref=rbuf.at[hi, t], send_sem=fss.at[t], recv_sem=frs.at[hi, t],
            device_id=owner(t), device_id_type=MESH)

    def tile(i, carry):
        rows = pl.ds(pl.multiple_of(i * 256, 256), 256)
        a = jnp.concatenate([cbuf[t // 2, t % 2, h, rows, :] for t in range(8) for h in range(3)], axis=1)
        s = jnp.dot(a, wv[...].reshape(3072, 768), preferred_element_type=F32).astype(BF16)
        for q in range(4):
            t = i * 4 + q
            part[t] = s[q * 64:q * 64 + 64, :]

            @pl.when(t == col)
            def _():
                rbuf[x_hi, slab] = s[q * 64:q * 64 + 64, :]

            @pl.when(t != col)
            def _():
                send(t).start()
        return carry

    lax.fori_loop(0, 4, tile, 0)
    for t in range(8):
        for hi in range(2):
            @pl.when(hi * 8 + t != col)
            def _():
                arrival(hi, t).wait_recv()
        out[:, t * 768:t * 768 + 768] = (rbuf[0, t].astype(F32) + rbuf[1, t].astype(F32)).astype(BF16)
    for slot in range(4):
        ring(slot, False).wait_send()
    for k in range(5):
        across(k, False).wait_send()
    for t in range(16):
        @pl.when(t != col)
        def _():
            send(t).wait_send()


def finish(ctx, wslab):
    vm = pl.BlockSpec(memory_space=pltpu.VMEM)
    anym = pl.BlockSpec(memory_space=pl.ANY)
    dma = pltpu.SemaphoreType.DMA
    return pl.pallas_call(
        finish_kernel,
        out_shape=jax.ShapeDtypeStruct((64, 6144), BF16),
        in_specs=[anym, anym],
        out_specs=vm,
        scratch_shapes=[
            pltpu.VMEM((4, 2, 3, 1024, 128), BF16),
            pltpu.VMEM((8, 384, 768), BF16),
            pltpu.VMEM((16, 64, 768), BF16),
            pltpu.VMEM((2, 8, 64, 768), BF16),
            dma((4,)), dma((4,)), dma((5,)), dma((5,)), dma((16,)), dma((2, 8)), dma((1,)), dma((2,)),
        ],
        compiler_params=pltpu.CompilerParams(collective_id=2, has_side_effects=True, vmem_limit_bytes=VMEM_LIMIT),
        name="finish",
    )(ctx, wslab)


def local(patches, w_patch, patch_bias, ln_gain, w_qkv, qk_gain, w_out):
    p2d = patches.reshape(64, 768)
    pown = p2d.reshape(2, 32, 3, 256).transpose(2, 0, 1, 3)
    bias = patch_bias.astype(F32)[None, :]
    gain = ln_gain.astype(F32)[None, :]
    buf, rs, w, rpos, cpos = prep(pown, p2d, bias, gain, w_patch, w_qkv.transpose(1, 2, 0, 3))
    ctx, wslab = attend(buf, rs, w, rpos, cpos, qk_gain, w_out.reshape(384, 768))
    return finish(ctx, wslab)


def solution(mesh):
    return jax.shard_map(
        local,
        mesh=mesh,
        in_specs=(
            P("row", "col", None), P(), P(), P(),
            P(None, None, "col", None), P(None, "col", None), P("col", None, "row"),
        ),
        out_specs=P(("row", "col"), None),
        check_vma=False,
    )
```

time: 728 us -> 235 us (0.32)
  waiting for transfers between devices: 429 us -> 0 us
  Pallas kernels: 0 us -> 224 us
  matrix products: 141 us -> 0 us
  local copies, waits for them, and re-layouts: 78.8 us -> 4.92 us
  other arithmetic: 61.9 us -> 2.62 us
  between operations: 13.3 us -> 0.03 us
    all_gather x4 -> x0, waiting for transfers between devices: 306 us -> none  [the longest x1 122 us: local(): key_piece = lax.all_gather(keys_here, 'row', axis=0, tiled=True)]
    pallas_call x0 -> x3, Pallas kernels: none -> 224 us  [the longest x1 105 us: attend(): pl.pallas_call(attend_kernel, out_shape=(jax.ShapeDtypeStruct((3, 1024, 1...]
    dot_general x19 -> x0, matrix products: 141 us -> none  [the longest x8 62 us: step_block(): jnp.einsum('hqd,khd->hqk', query_heads, block_keys, preferred_element_typ...]
    reduce_scatter x1 -> x0, waiting for transfers between devices: 123 us -> none  [local(): lax.psum_scatter(jnp.dot(context, out_weight, preferred_element_type=jnp....]
    unnamed x17 -> x2, local copies, waits for them, and re-layouts: 65.4 us -> 3.34 us
    reduce_sum x11 -> x0, other arithmetic: 55.5 us -> none  [the longest x8 54.5 us: step_block(): new_total = run_total * rescale + jnp.sum(exponent, axis=2)]
    while x24 -> x0, local copies, waits for them, and re-layouts: 10.9 us -> none
  transfers between devices with their start and end apart: 5 -> 0, of which waited for: 4 -> 0; matrix products, arithmetic and copies ran while one was open for 31% -> 0% of each run, Pallas kernels for 0% -> 0%
where the time goes in v1:
time: 235 us; the launch traced here: 232 us
  Pallas kernels  224 us (95%)
  local copies, waits for them, and re-layouts  4.92 us (2%)
  other arithmetic  2.62 us (1%)
    pallas_call x1, Pallas kernels, attend(): pl.pallas_call(attend_kernel, out_shape=(jax.ShapeDtypeStruct((3, 1024, 1...  105 us
    pallas_call x1, Pallas kernels, prep(): pl.pallas_call(prep_kernel, out_shape=(jax.ShapeDtypeStruct((3, 4, 4, 4,...  60.1 us
    pallas_call x1, Pallas kernels, finish(): pl.pallas_call(finish_kernel, out_shape=jax.ShapeDtypeStruct((64, 6144),...  59 us

profile of v1, /device:TPU:25, one launch (start us, length us, event | category | flops | bytes accessed | tf_op | source)
XLA Modules:
  0.0 231.7 jit_solution(10298907680295490519)
XLA Ops:
  0.0 1.3 copy.14.qk_gain
  1.3 1.3 broadcast_in_dim.14
  2.6 1.3 broadcast_in_dim.15
  3.9 0.9 reshape_reshape.3
  4.8 0.7 copy.16
  5.5 60.1 %prep.1 = (bf16[3,4,4,4,2,2,32,256]{7,6,5,4,3,2,1,0:T(8,128)(2,1)}, f32[4,4,4,2,1,128]{5,4,3,2,1,0:T(1,128)}, bf16[768,1152]{1,0:T(8,128)(2,1)}, f32[64,1152]{1,0:T(8,128)}, f32[128,1152]{1,0:T(8,128)}) custom-call(bf16[3,2,32,256]{3,2,1,0:T(8,128)(2,1)} %bitcast.11, bf16[64,768]{1,0:T(8,128)(2,1)} %bitcast.10, f32[1,6144]{1,0:T(1,128)} %bitcast.12, ...), custom_call_target="tpu_custom_call" | custom-call | tf_op jit(solution)/shard_map/prep/pallas_call | solution.py:315
  65.6 105.0 %attend.1 = (bf16[3,1024,128]{2,1,0:T(8,128)(2,1)}, bf16[8,384,768]{2,1,0:T(8,128)(2,1)}) custom-call(bf16[3,4,4,4,2,2,32,256]{7,6,5,4,3,2,1,0:T(8,128)(2,1)} %get-tuple-element.12.buf, f32[4,4,4,2,1,128]{5,4,3,2,1,0:T(1,128)} %get-tuple-element.13.rs_ref, bf16[768,1152]{1,0:T(8,128)(2,1)} %get-tuple-element.14.w_ref, f32[64,1152]{1,0:T(8,128)} %get-tuple-element.15.rpos, ...), custom_call_target="tpu_custom_call" | custom-call | tf_op jit(solution)/shard_map/attend/pallas_call | solution.py:509
  170.6 59.0 %finish.1 = bf16[64,6144]{1,0:T(8,128)(2,1)} custom-call(bf16[3,1024,128]{2,1,0:T(8,128)(2,1)} %get-tuple-element.17.ctx, bf16[8,384,768]{2,1,0:T(8,128)(2,1)} %get-tuple-element.18.wslab_hbm), custom_call_target="tpu_custom_call" | custom-call | tf_op jit(solution)/shard_map/finish/pallas_call | solution.py:650
  229.6 2.1 copy.18

commit v2 on v0

v2 whole, which is shorter than its diff:
```python
import math

import numpy as np
import jax
import jax.numpy as jnp
from jax import lax
from jax.experimental import pallas as pl
from jax.experimental.pallas import tpu as pltpu
from jax.sharding import PartitionSpec as P

NORM_EPS = 1e-06
MESH = pl.DeviceIdType.MESH
F32 = jnp.float32
BF16 = jnp.bfloat16
ORDERS = ((0, 1, 2), (1, 2, 0), (2, 0, 1))
LHS_ROWS = 992
ROW_C, ROW_R, ROW_BIAS, ROW_GAIN = 768, 896, 960, 961
VMEM_LIMIT = 67043328
QT, CHAINS = 256, 2


def device(x, y, z, c):
    return (y * 2 + x % 2, (x // 2) * 8 + z * 2 + c)


def trig_tables():
    quarter = 1536
    freq = 10000.0 ** (-np.arange(quarter, dtype=np.float64) / quarter)
    coarse = 8.0 * np.arange(16, dtype=np.float64)[:, None] * freq[None, :]
    fine = np.arange(8, dtype=np.float64)[:, None] * freq[None, :]
    f = lambda a: a.astype(np.float32)
    return f(np.sin(coarse)), f(np.cos(coarse)), f(np.sin(fine)), f(np.cos(fine))


def fused_kernel(
    bg, qk_gain, sa, ca, sb, cb, p_hbm, wp_hbm, wq_hbm, wo_hbm,
    out, buf,
    p2d, rsbuf, rsown, wres, rpos, cpos, cbuf, wslab, part, rbuf,
    ssem, rsem, pss, prs, xss, xrs, lsem, wsem, osem,
    w1s, w1r, wxs, wxr, wrs, wrr,
    css, crs, dss, drs, fss, frs, tsem,
):
    row = lax.axis_index("row")
    col = lax.axis_index("col")
    x = (col // 8) * 2 + row % 2
    y = row // 2
    z = (col // 2) % 4
    c = col % 2
    x_hi, x_lo = x // 2, x % 2
    coord = (x, y, z)

    def near(axis, d):
        t = list(coord)
        t[axis] = (t[axis] + d) % 4
        return device(t[0], t[1], t[2], c)

    partner = device(x, y, z, 1 - c)

    def remote(src, dst, send, recv, to):
        return pltpu.make_async_remote_copy(
            src_ref=src, dst_ref=dst, send_sem=send, recv_sem=recv, device_id=to, device_id_type=MESH)

    def piece(p, ph, val, core, half=None):
        order = ORDERS[p]
        idx = []
        for b in range(3):
            if b in order[:ph]:
                idx.append(pl.ds(0, 4))
            elif b == order[ph]:
                idx.append(val)
            else:
                idx.append(coord[b])
        tail = () if half is None else (pl.ds(half * 32, 32),)
        return buf.at[(p, *idx, core, *tail)]

    SLOTS = ((0, 1), (1, 3), (1, 1), (0, 3), (0, 1), (1, 3))

    def ring(p, ph, slot, recv):
        axis = ORDERS[p][ph]
        own = coord[axis]
        half, d = SLOTS[slot]
        if slot < 4:
            if recv:
                src = dst = piece(p, ph, (own + 4 - d) % 4, c, half)
            else:
                dst = piece(p, ph, own, c, half)
                src = p_hbm.at[pl.ds(half * 32, 32), pl.ds(p * 256, 256)] if ph == 0 else dst
        else:
            src = dst = piece(p, ph, (own + (2 if recv else 4 - d)) % 4, c, half)
        return remote(src, dst, ssem.at[p, ph, slot], rsem.at[p, ph, slot], near(axis, d))

    def across(p, k, recv):
        core = 1 - c if recv else c
        own = coord[ORDERS[p][2]]
        val = (own, (own + 3) % 4, (own + 1) % 4, (own + 2) % 4, (own + 2) % 4)[k]
        ref = piece(p, 2, val, core, None if k < 3 else k - 3)
        return remote(ref, ref, pss.at[p, k], prs.at[p, k], partner)

    def start_phase(ph):
        for slot in range(4):
            for p in range(3):
                ring(p, ph, slot, False).start()

    def forward_phase(ph):
        for slot in (0, 1):
            for p in range(3):
                ring(p, ph, slot, True).wait_recv()
                ring(p, ph, slot + 4, False).start()

    def direct_phase(ph):
        for slot in (2, 3):
            for p in range(3):
                ring(p, ph, slot, True).wait_recv()
                if ph == 2:
                    across(p, slot - 1, False).start()

    def finish_phase(ph):
        for slot in (4, 5):
            for p in range(3):
                ring(p, ph, slot, True).wait_recv()
                if ph == 2:
                    across(p, slot - 1, False).start()

    def rs_copy(step, d, recv):
        if step == 0:
            core = 1 - c if recv else c
            dst = rsbuf.at[x, y, z, core]
            src = dst if recv else rsown
            to = partner
        else:
            axis = step - 1
            idx = []
            for b in range(3):
                if b < axis:
                    idx.append(pl.ds(0, 4))
                elif b == axis:
                    idx.append((coord[b] + 4 - d) % 4 if recv else coord[b])
                else:
                    idx.append(coord[b])
            src = dst = rsbuf.at[tuple(idx)]
            to = near(axis, d)
        return remote(src, dst, xss.at[step, d], xrs.at[step, d], to)

    def rs_step(step):
        for d in ((0,) if step == 0 else (1, 2, 3)):
            rs_copy(step, d, False).start()

    def rs_wait(step):
        for d in ((0,) if step == 0 else (1, 2, 3)):
            rs_copy(step, d, True).wait_recv()

    stays = (y == z) & (c == x_lo)
    w1_to = device(x_hi * 2 + c, z, y, x_lo)

    def w1(recv):
        dst = wslab.at[row] if recv else wslab.at[z * 2 + c]
        return remote(wo_hbm, dst, w1s, w1r, w1_to)

    def w1_local():
        return pltpu.make_async_copy(wo_hbm, wslab.at[row], w1r)

    x_pair = device(x_hi * 2 + 1 - x_lo, y, z, c)

    def wx(recv):
        ref = wslab.at[y * 2 + 1 - x_lo] if recv else wslab.at[row]
        return remote(ref, ref, wxs, wxr, x_pair)

    def wring(which, slot, recv):
        lo = x_lo if which == 0 else 1 - x_lo
        half, d = SLOTS[slot]
        if slot < 4:
            ref = wslab.at[((y + (4 - d if recv else 0)) % 4) * 2 + lo, half]
        else:
            ref = wslab.at[((y + (2 if recv else 4 - d)) % 4) * 2 + lo, half]
        return remote(ref, ref, wrs.at[which, slot], wrr.at[which, slot], near(1, d))

    def wring_start(which):
        for slot in range(4):
            wring(which, slot, False).start()

    def wring_forward(which):
        for slot in (0, 1):
            wring(which, slot, True).wait_recv()
            wring(which, slot + 4, False).start()

    def wring_finish(which):
        for slot in range(2, 6):
            wring(which, slot, True).wait_recv()

    def cring(u, slot, recv):
        h, half = u % 3, u // 3
        d = 1 if slot % 2 == 0 else 3
        if slot < 2:
            ref = cbuf.at[half, h, (z + (4 - d if recv else 0)) % 4, c]
        else:
            ref = cbuf.at[half, h, (z + (2 if recv else 4 - d)) % 4, c, pl.ds((slot - 2) * 256, 256)]
        return remote(ref, ref, css.at[u, slot], crs.at[u, slot], near(2, d))

    def cacross(u, k, recv):
        h, half = u % 3, u // 3
        core = 1 - c if recv else c
        if k < 3:
            ref = cbuf.at[half, h, (z + (0, 3, 1)[k]) % 4, core]
        else:
            ref = cbuf.at[half, h, (z + 2) % 4, core, pl.ds((k - 3) * 256, 256)]
        return remote(ref, ref, dss.at[u, k], drs.at[u, k], partner)

    def ctx_start(u):
        cring(u, 0, False).start()
        cring(u, 1, False).start()
        cacross(u, 0, False).start()

    def ctx_forward(u):
        for slot in (0, 1):
            cring(u, slot, True).wait_recv()
            cring(u, slot + 2, False).start()
            cacross(u, 1 + slot, False).start()

    def ctx_finish(u):
        for slot in (2, 3):
            cring(u, slot, True).wait_recv()
            cacross(u, 1 + slot, False).start()

    def ctx_ready(u):
        for k in range(5):
            cacross(u, k, True).wait_recv()

    slab = z * 2 + c

    def owner(half, t):
        return (t // 4) * 8 + (t % 4) * 2 + half

    def send(half, t):
        return remote(part.at[half * 8 + t], rbuf.at[x_hi, slab], fss.at[half * 8 + t], frs.at[x_hi, slab],
                      (row, owner(half, t)))

    def arrival(hi, t):
        return remote(part.at[0], rbuf.at[hi, t], fss.at[0], frs.at[hi, t], (row, hi * 8 + t))

    p_copy = pltpu.make_async_copy(p_hbm, p2d, osem.at[2])
    p_copy.start()

    barrier = pltpu.get_barrier_semaphore()
    peers = [near(a, d) for a in range(3) for d in (1, 2, 3)] + [partner]
    for peer in peers:
        pl.semaphore_signal(barrier, inc=1, device_id=peer, device_id_type=MESH)

    @pl.when(jnp.logical_not(stays))
    def _():
        pl.semaphore_signal(barrier, inc=1, device_id=w1_to, device_id_type=MESH)
    for t in range(16):
        @pl.when(col != t)
        def _():
            pl.semaphore_signal(barrier, inc=1, device_id=(row, t), device_id_type=MESH)

    def prepare(lhs, wq, emb, res, mu):
        wp = lhs
        wp_copies = [
            pltpu.make_async_copy(wp_hbm.at[pl.ds(i * 192, 192)], wp.at[pl.ds(i * 192, 192)], lsem.at[i])
            for i in range(4)]
        for cp in wp_copies:
            cp.start()
        wq_copies = [pltpu.make_async_copy(wq_hbm.at[b // 3, b % 3], wq.at[b], wsem.at[b]) for b in range(9)]
        for cp in wq_copies:
            cp.start()

        pl.semaphore_wait(barrier, jnp.where(stays, len(peers) + 15, len(peers) + 16))
        start_phase(0)

        @pl.when(stays)
        def _():
            w1_local().start()

        @pl.when(jnp.logical_not(stays))
        def _():
            w1(False).start()
        p_copy.wait()
        own_copies = [
            pltpu.make_async_copy(p2d.at[:, pl.ds(p * 256, 256)], buf.at[p, x, y, z, c], osem.at[3 + p])
            for p in range(3)]
        for cp in own_copies:
            cp.start()

        gain = bg[1:2, :]
        gain_lo, gain_hi = gain[:, :3072], gain[:, 3072:]
        bias = bg[0:1, :]

        lhs[ROW_C:ROW_C + 128, 0:3072] = jnp.zeros((128, 3072), BF16)
        lhs[ROW_R:ROW_R + 64, 3072:6144] = jnp.zeros((64, 3072), BF16)
        sbv, cbv = sb[...], cb[...]
        for t in range(8):
            sins, coss = [], []
            for u in (2 * t, 2 * t + 1):
                sav, cav = sa[u:u + 1, :], ca[u:u + 1, :]
                sins.append(sav * cbv + cav * sbv)
                coss.append(cav * cbv - sav * sbv)
            table = jnp.concatenate([jnp.concatenate(sins, 0), jnp.concatenate(coss, 0)], axis=1)
            mu[16 * t:16 * t + 16, :] = jnp.broadcast_to(
                jnp.sum(table, axis=1, keepdims=True) * (1.0 / 6144), (16, 128))
            lhs[ROW_C + 16 * t:ROW_C + 16 * t + 16, 3072:6144] = (table * gain_hi).astype(BF16)
            if t < 4:
                lhs[ROW_R + 16 * t:ROW_R + 16 * t + 16, 0:3072] = (table * gain_lo).astype(BF16)
        bias_c = (bias - jnp.mean(bias, axis=1, keepdims=True)) * gain
        tail_rows = lax.broadcasted_iota(jnp.int32, (32, 6144), 0)
        lhs[ROW_BIAS:ROW_BIAS + 32, :] = jnp.where(
            tail_rows == 0, bias_c, jnp.where(tail_rows == 1, gain, 0.0)).astype(BF16)

        for cp in wp_copies:
            cp.wait()
        forward_phase(0)

        def own_table(n):
            sav, cav = sa[pl.ds(n, 1), :], ca[pl.ds(n, 1), :]
            return jnp.concatenate([sav * cbv + cav * sbv, cav * cbv - sav * sbv], axis=1)

        t_row, t_col = own_table(row), own_table(col)
        pixels = p2d[...]
        total = jnp.zeros((64, 1), F32)
        for n in range(12):
            lo = n * 512
            e = jnp.dot(pixels, wp[0:768, lo:lo + 512], preferred_element_type=F32) + bias[:, lo:lo + 512]
            e = e.reshape(8, 8, 512)
            if n < 6:
                e = e + t_row[:, lo:lo + 512].reshape(8, 1, 512)
            else:
                e = e + t_col[:, lo - 3072:lo - 2560].reshape(1, 8, 512)
            e = e.reshape(64, 512)
            emb[:, lo:lo + 512] = e
            total = total + jnp.sum(e, axis=1, keepdims=True)
        for cp in own_copies:
            cp.wait()
        direct_phase(0)
        finish_phase(0)
        start_phase(1)
        mean = total * (1.0 / 6144)
        square = jnp.zeros((64, 1), F32)
        for n in range(12):
            d = emb[:, n * 512:n * 512 + 512] - mean
            square = square + jnp.sum(d * d, axis=1, keepdims=True)
        rstd = lax.rsqrt(square * (1.0 / 6144) + NORM_EPS)
        rs_wide = jnp.concatenate([jnp.broadcast_to(rstd, (64, 128)), jnp.zeros((64, 128), F32)], axis=0)
        rsown[...] = rs_wide.T[0:1, :]
        rs_own_copy = pltpu.make_async_copy(rsown, rsbuf.at[x, y, z, c], osem.at[1])
        rs_own_copy.start()
        rs_step(0)

        def center(i, carry):
            w = wp[pl.ds(pl.multiple_of(i * 48, 48), 48), :].astype(F32)
            w = (w - jnp.mean(w, axis=1, keepdims=True)) * gain
            lhs[pl.ds(pl.multiple_of(i * 48, 48), 48), :] = w.astype(BF16)
            return carry

        lax.fori_loop(0, 8, center, 0)
        forward_phase(1)
        rs_own_copy.wait()
        rs_wait(0)
        rs_step(1)
        lax.fori_loop(8, 16, center, 0)
        direct_phase(1)
        finish_phase(1)
        start_phase(2)
        for p in range(3):
            across(p, 0, False).start()
        rs_wait(1)
        rs_step(2)
        for cp in wq_copies:
            cp.wait()

        def product(it, carry):
            pair = it // 2
            rows = pl.ds(pl.multiple_of((it % 2) * 496, 496), 496)
            second = jnp.minimum(2 * pair + 1, 8)
            w = jnp.concatenate([wq[2 * pair], wq[second]], axis=1)
            res[pair, rows, :] = jnp.dot(lhs[rows, :], w, preferred_element_type=F32)

            @pl.when(it == 2)
            def _():
                rs_wait(2)
                rs_step(3)

            @pl.when(it == 5)
            def _():
                forward_phase(2)

            @pl.when(it == 8)
            def _():
                direct_phase(2)
            return carry

        lax.fori_loop(0, 10, product, 0)

        mus = mu[...]
        for b in range(9):
            lanes = slice((b % 2) * 128, (b % 2) * 128 + 128)
            w = res[b // 2, 0:768, lanes]
            gsum = res[b // 2, ROW_GAIN:ROW_GAIN + 1, lanes]
            rp = res[b // 2, ROW_R:ROW_R + 64, lanes] - mus[:64] * gsum + res[b // 2, ROW_BIAS:ROW_BIAS + 1, lanes]
            cp = res[b // 2, ROW_C:ROW_C + 128, lanes] - mus * gsum
            if b < 6:
                w = w - jnp.mean(w, axis=1, keepdims=True)
                rp = rp - jnp.mean(rp, axis=1, keepdims=True)
                cp = cp - jnp.mean(cp, axis=1, keepdims=True)
            lanes = slice(b * 128, b * 128 + 128)
            wres[:, lanes] = w.astype(BF16)
            rpos[:, lanes] = rp
            cpos[:, lanes] = cp
        finish_phase(2)
        rs_wait(3)

        @pl.when(stays)
        def _():
            w1_local().wait()

        @pl.when(jnp.logical_not(stays))
        def _():
            w1(True).wait_recv()
        wx(False).start()
        wring_start(0)
        for p in range(3):
            for k in range(5):
                across(p, k, True).wait_recv()

    pl.run_scoped(
        prepare,
        pltpu.VMEM((LHS_ROWS, 6144), BF16),
        pltpu.VMEM((9, 6144, 128), BF16),
        pltpu.VMEM((64, 6144), F32),
        pltpu.VMEM((5, LHS_ROWS, 256), F32),
        pltpu.VMEM((128, 128), F32),
    )

    def attend(tiles, kall, vall, qall):
        def tile_copies(n, slot):
            return [
                pltpu.make_async_copy(buf.at[p, n // 4, n % 4], tiles.at[slot, p], tsem.at[slot, p])
                for p in range(3)]

        scale = math.log2(math.e) / math.sqrt(128.0)

        def project(n, slot, first, width):
            cx, cy = n // 4, n % 4
            p = jnp.concatenate([tiles[slot, q].reshape(512, 256) for q in range(3)], axis=1)
            yv = jnp.dot(p, wres[:, first:first + width], preferred_element_type=F32).reshape(8, 8, 8, width)
            r = cy * 2 + cx % 2
            rp = rpos[pl.ds(pl.multiple_of(r * 8, 8), 8), first:first + width]
            cp = cpos[pl.ds(pl.multiple_of((cx // 2) * 64, 64), 64), first:first + width]
            yv = yv + rp.reshape(1, 8, 1, width) + cp.reshape(8, 1, 8, width)
            rst = jnp.concatenate([rsbuf[cx, cy].reshape(8, 128), jnp.zeros((120, 128), F32)], axis=0).T
            rcol = jnp.concatenate([rst[0:64, q:q + 1] for q in range(8)], axis=0)
            return yv.reshape(512, width), rcol

        def normed(yh, rcol, gain):
            var = jnp.mean(yh * yh, axis=1, keepdims=True)
            return yh * (rcol * lax.rsqrt(rcol * rcol * var + NORM_EPS)) * gain

        for cp in tile_copies(0, 0):
            cp.start()

        def fill(n, carry):
            slot = n % 2

            @pl.when(n + 1 < 16)
            def _():
                for cp in tile_copies(n + 1, 1 - slot):
                    cp.start()
            for cp in tile_copies(n, slot):
                cp.wait()
            yv, rcol = project(n, slot, 384, 768)
            at = pl.ds(pl.multiple_of(n * 512, 512), 512)
            for h in range(3):
                kall[h, at, :] = normed(yv[:, h * 128:h * 128 + 128], rcol, qk_gain[h, 1:2, :]).astype(BF16)
                vall[h, at, :] = (yv[:, 384 + h * 128:512 + h * 128] * rcol).astype(BF16)

            @pl.when((n % 4 == y) & ((n // 4) % 2 == x_lo))
            def _():
                yq, rq = project(n, slot, 0, 384)
                for h in range(3):
                    qh = normed(yq[:, h * 128:h * 128 + 128], rq, qk_gain[h, 0:1, :] * scale).reshape(8, 8, 8, 128)
                    for i in range(8):
                        dst = (n // 8) * 512 + i * 64
                        qall[h, pl.ds(pl.multiple_of(dst, 64), 64), :] = qh[:, i].reshape(64, 128).astype(BF16)

            @pl.when(n == 12)
            def _():
                wring_forward(0)
                wx(True).wait_recv()
                wring_start(1)
            return carry

        lax.fori_loop(0, 16, fill, 0)

        ones = jnp.ones((8192, 128), BF16)

        def partial_rows(half, i, heads):
            rows = pl.ds(pl.multiple_of(i * 256, 256), 256)
            total = None
            for h in heads:
                a = jnp.concatenate([cbuf[half, h, t // 2, t % 2, rows, :] for t in range(8)], axis=1)
                w = jnp.concatenate(
                    [wslab[t, h * 128 // 192, (h * 128) % 192:(h * 128) % 192 + 128, :] if h != 1 else
                     jnp.concatenate([wslab[t, 0, 128:192, :], wslab[t, 1, 0:64, :]], axis=0) for t in range(8)], axis=0)
                d = jnp.dot(a, w, preferred_element_type=F32)
                total = d if total is None else total + d
            return total

        def ship(half, i, rows):
            for q in range(4):
                t = i * 4 + q
                part[half * 8 + t] = rows[q * 64:q * 64 + 64, :]

                @pl.when(owner(half, t) == col)
                def _():
                    rbuf[x_hi, slab] = rows[q * 64:q * 64 + 64, :]

                @pl.when(owner(half, t) != col)
                def _():
                    send(half, t).start()

        def unit(u, carry):
            h, half = u % 3, u // 3
            k = kall[h]
            va = jnp.concatenate([vall[h], ones], axis=1)
            scores = [
                lax.dot_general(
                    qall[h, pl.ds(pl.multiple_of(half * 512 + t * QT, QT), QT), :], k,
                    (((1,), (1,)), ((), ())), preferred_element_type=F32)
                for t in range(CHAINS)]
            for t in range(CHAINS):
                p = jnp.exp2(scores[t] - jnp.max(scores[t], axis=1, keepdims=True)).astype(BF16)
                a = jnp.dot(p, va, preferred_element_type=F32)
                cbuf[half, h, z, c, t * QT:t * QT + QT, :] = (a[:, :128] / a[:, 128:]).astype(BF16)

            @pl.when(u >= 2)
            def _():
                ctx_finish(u - 2)

            @pl.when(u >= 1)
            def _():
                ctx_forward(u - 1)
            ctx_start(u)

            @pl.when(u == 1)
            def _():
                wring_forward(1)

            @pl.when(u == 4)
            def _():
                wring_finish(0)
                wring_finish(1)
                for v in range(3):
                    ctx_ready(v)

                def tile(i, carry2):
                    ship(0, i, partial_rows(0, i, (0, 1, 2)).astype(BF16))
                    return carry2
                lax.fori_loop(0, 2, tile, 0)
            return carry

        lax.fori_loop(0, 6, unit, 0)
        ctx_finish(4)
        for v in (3, 4):
            ctx_ready(v)
        ctx_forward(5)
        ctx_finish(5)
        ctx_ready(5)

        def last_tile(i, carry):
            ship(1, i, partial_rows(1, i, (0, 1, 2)).astype(BF16))
            return carry
        lax.fori_loop(0, 2, last_tile, 0)

    pl.run_scoped(
        attend,
        pltpu.VMEM((2, 3, 4, 2, 64, 256), BF16),
        pltpu.VMEM((3, 8192, 128), BF16),
        pltpu.VMEM((3, 8192, 128), BF16),
        pltpu.VMEM((3, 1024, 128), BF16),
    )

    for t in range(8):
        for hi in range(2):
            @pl.when(hi * 8 + t != col)
            def _():
                arrival(hi, t).wait_recv()
        out[:, t * 768:t * 768 + 768] = (rbuf[0, t].astype(F32) + rbuf[1, t].astype(F32)).astype(BF16)

    for p in range(3):
        for ph in range(3):
            for slot in range(6):
                ring(p, ph, slot, False).wait_send()
        for k in range(5):
            across(p, k, False).wait_send()
    for step in range(4):
        for d in ((0,) if step == 0 else (1, 2, 3)):
            rs_copy(step, d, False).wait_send()

    @pl.when(jnp.logical_not(stays))
    def _():
        w1(False).wait_send()
    wx(False).wait_send()
    for which in range(2):
        for slot in range(6):
            wring(which, slot, False).wait_send()

    for u in range(6):
        for slot in range(4):
            cring(u, slot, False).wait_send()
        for k in range(5):
            cacross(u, k, False).wait_send()
    for half in range(2):
        for t in range(8):
            @pl.when(owner(half, t) != col)
            def _():
                send(half, t).wait_send()


def fused(bg, qk_gain, patches, w_patch, w_qkv, w_out):
    tables = [jnp.asarray(t) for t in trig_tables()]
    vm = pl.BlockSpec(memory_space=pltpu.VMEM)
    anym = pl.BlockSpec(memory_space=pl.ANY)
    dma = pltpu.SemaphoreType.DMA
    return pl.pallas_call(
        fused_kernel,
        out_shape=(
            jax.ShapeDtypeStruct((64, 6144), BF16),
            jax.ShapeDtypeStruct((3, 4, 4, 4, 2, 64, 256), BF16),
        ),
        in_specs=[vm] * 6 + [anym] * 4,
        out_specs=(vm, anym),
        scratch_shapes=[
            pltpu.VMEM((64, 768), BF16),
            pltpu.VMEM((4, 4, 4, 2, 1, 128), F32),
            pltpu.VMEM((1, 128), F32),
            pltpu.VMEM((768, 1152), BF16),
            pltpu.VMEM((64, 1152), F32),
            pltpu.VMEM((128, 1152), F32),
            pltpu.VMEM((2, 3, 4, 2, 512, 128), BF16),
            pltpu.VMEM((8, 2, 192, 768), BF16),
            pltpu.VMEM((16, 64, 768), BF16),
            pltpu.VMEM((2, 8, 64, 768), BF16),
            dma((3, 3, 6)), dma((3, 3, 6)), dma((3, 5)), dma((3, 5)),
            dma((4, 4)), dma((4, 4)), dma((4,)), dma((9,)), dma((6,)),
            dma, dma, dma, dma, dma((2, 6)), dma((2, 6)),
            dma((6, 4)), dma((6, 4)), dma((6, 5)), dma((6, 5)), dma((16,)), dma((2, 8)), dma((2, 3)),
        ],
        compiler_params=pltpu.CompilerParams(collective_id=0, has_side_effects=True, vmem_limit_bytes=VMEM_LIMIT),
        name="fused",
    )(bg, qk_gain, *tables, patches, w_patch, w_qkv, w_out)


def local(patches, w_patch, patch_bias, ln_gain, w_qkv, qk_gain, w_out):
    bg = jnp.stack([patch_bias, ln_gain]).astype(F32)
    out, _ = fused(
        bg, qk_gain.transpose(1, 0, 2), patches.reshape(64, 768), w_patch,
        w_qkv.transpose(1, 2, 0, 3), w_out.reshape(2, 192, 768))
    return out


def solution(mesh):
    return jax.shard_map(
        local,
        mesh=mesh,
        in_specs=(
            P("row", "col", None), P(), P(), P(),
            P(None, None, "col", None), P(None, "col", None), P("col", None, "row"),
        ),
        out_specs=P(("row", "col"), None),
        check_vma=False,
    )
```

time: 728 us -> 182 us (0.25)
  waiting for transfers between devices: 429 us -> 0 us
  Pallas kernels: 0 us -> 175 us
  matrix products: 141 us -> 0 us
  local copies, waits for them, and re-layouts: 78.8 us -> 3.51 us
  other arithmetic: 61.9 us -> 0.68 us
  between operations: 13.3 us -> 0.02 us
    all_gather x4 -> x0, waiting for transfers between devices: 306 us -> none  [the longest x1 122 us: local(): key_piece = lax.all_gather(keys_here, 'row', axis=0, tiled=True)]
    pallas_call x0 -> x1, Pallas kernels: none -> 175 us  [fused(): pl.pallas_call(fused_kernel, out_shape=(jax.ShapeDtypeStruct((64, 6144),...]
    dot_general x19 -> x0, matrix products: 141 us -> none  [the longest x8 62 us: step_block(): jnp.einsum('hqd,khd->hqk', query_heads, block_keys, preferred_element_typ...]
    reduce_scatter x1 -> x0, waiting for transfers between devices: 123 us -> none  [local(): lax.psum_scatter(jnp.dot(context, out_weight, preferred_element_type=jnp....]
    unnamed x17 -> x1, local copies, waits for them, and re-layouts: 65.4 us -> 2.06 us
    reduce_sum x11 -> x0, other arithmetic: 55.5 us -> none  [the longest x8 54.5 us: step_block(): new_total = run_total * rescale + jnp.sum(exponent, axis=2)]
    while x24 -> x0, local copies, waits for them, and re-layouts: 10.9 us -> none
  transfers between devices with their start and end apart: 5 -> 0, of which waited for: 4 -> 0; matrix products, arithmetic and copies ran while one was open for 31% -> 0% of each run, Pallas kernels for 0% -> 0%
where the time goes in v2:
time: 182 us; the launch traced here: 179 us
  Pallas kernels  175 us (96%)
  local copies, waits for them, and re-layouts  3.51 us (2%)
    pallas_call x1, Pallas kernels, fused(): pl.pallas_call(fused_kernel, out_shape=(jax.ShapeDtypeStruct((64, 6144),...  175 us

profile of v2, /device:TPU:25, one launch (start us, length us, event | category | flops | bytes accessed | tf_op | source)
XLA Modules:
  0.0 179.1 jit_solution(3520600642623664573)
XLA Ops:
  0.0 0.7 stack.9
  0.7 0.7 stack.10
  1.5 0.7 maximum_convert_fusion.bg
  2.1 174.9 %fused.1 = (bf16[64,6144]{1,0:T(8,128)(2,1)}, bf16[3,4,4,4,2,64,256]{6,5,4,3,2,1,0:T(8,128)(2,1)}) custom-call(f32[2,6144]{1,0:T(2,128)} %maximum_convert_fusion.bg, f32[3,2,128]{2,1,0:T(2,128)} %bitcast.7, f32[16,1536]{1,0:T(8,128)} %constant.8.clone.sa, f32[16,1536]{1,0:T(8,128)} %constant.9.clone.ca, f32[8,1536]{1,0:T(8,128)} %constant.10.clone.sb, ...), custom_call_target="tpu_custom_call" | custom-call | tf_op jit(solution)/shard_map/fused/pallas_call | solution.py:622
  177.1 2.1 %copy.13 = bf16[64,6144]{1,0:T(8,128)(2,1)} copy(bf16[64,6144]{1,0:T(8,128)(2,1)} %get-tuple-element.6) | data formatting | bytes 1572864

commit v3 on v2

--- a/solution.py
+++ b/solution.py
@@ -13,10 +13,10 @@
 F32 = jnp.float32
 BF16 = jnp.bfloat16
 ORDERS = ((0, 1, 2), (1, 2, 0), (2, 0, 1))
-LHS_ROWS = 992
+LHS_ROWS, LHS_TILE = 1008, 336
 ROW_C, ROW_R, ROW_BIAS, ROW_GAIN = 768, 896, 960, 961
 VMEM_LIMIT = 67043328
-QT, CHAINS = 256, 2
+QT = 128
 
 
 def device(x, y, z, c):
@@ -38,7 +38,7 @@
     p2d, rsbuf, rsown, wres, rpos, cpos, cbuf, wslab, part, rbuf,
     ssem, rsem, pss, prs, xss, xrs, lsem, wsem, osem,
     w1s, w1r, wxs, wxr, wrs, wrr,
-    css, crs, dss, drs, fss, frs, tsem,
+    css, crs, dss, drs, fss, frs, tsem, uss, urs,
 ):
     row = lax.axis_index("row")
     col = lax.axis_index("col")
@@ -75,19 +75,31 @@
 
     SLOTS = ((0, 1), (1, 3), (1, 1), (0, 3), (0, 1), (1, 3))
 
-    def ring(p, ph, slot, recv):
+    def cast(p, ph, d, recv):
         axis = ORDERS[p][ph]
+        dst = piece(p, ph, (coord[axis] + (4 - d if recv else 0)) % 4, c)
+        src = p_hbm.at[:, pl.ds(p * 256, 256)] if ph == 0 and not recv else dst
+        return remote(src, dst, uss.at[p, ph, d], urs.at[p, ph, d], near(axis, d))
+
+    def cast_start(ph):
+        for d in (1, 3, 2):
+            for p in range(3):
+                cast(p, ph, d, False).start()
+
+    def cast_wait(ph):
+        for d in (1, 3, 2):
+            for p in range(3):
+                cast(p, ph, d, True).wait_recv()
+
+    def ring(p, slot, recv):
+        axis = ORDERS[p][2]
         own = coord[axis]
         half, d = SLOTS[slot]
         if slot < 4:
-            if recv:
-                src = dst = piece(p, ph, (own + 4 - d) % 4, c, half)
-            else:
-                dst = piece(p, ph, own, c, half)
-                src = p_hbm.at[pl.ds(half * 32, 32), pl.ds(p * 256, 256)] if ph == 0 else dst
+            src = dst = piece(p, 2, (own + (4 - d if recv else 0)) % 4, c, half)
         else:
-            src = dst = piece(p, ph, (own + (2 if recv else 4 - d)) % 4, c, half)
-        return remote(src, dst, ssem.at[p, ph, slot], rsem.at[p, ph, slot], near(axis, d))
+            src = dst = piece(p, 2, (own + (2 if recv else 4 - d)) % 4, c, half)
+        return remote(src, dst, ssem.at[p, slot], rsem.at[p, slot], near(axis, d))
 
     def across(p, k, recv):
         core = 1 - c if recv else c
@@ -96,30 +108,33 @@
         ref = piece(p, 2, val, core, None if k < 3 else k - 3)
         return remote(ref, ref, pss.at[p, k], prs.at[p, k], partner)
 
-    def start_phase(ph):
+    def start_phase():
         for slot in range(4):
             for p in range(3):
-                ring(p, ph, slot, False).start()
-
-    def forward_phase(ph):
+                ring(p, slot, False).start()
+
+    def forward_phase():
         for slot in (0, 1):
             for p in range(3):
-                ring(p, ph, slot, True).wait_recv()
-                ring(p, ph, slot + 4, False).start()
-
-    def direct_phase(ph):
+                ring(p, slot, True).wait_recv()
+                ring(p, slot + 4, False).start()
+
+    def direct_phase():
         for slot in (2, 3):
             for p in range(3):
-                ring(p, ph, slot, True).wait_recv()
-                if ph == 2:
-                    across(p, slot - 1, False).start()
-
-    def finish_phase(ph):
+                ring(p, slot, True).wait_recv()
+                across(p, slot - 1, False).start()
+
+    def finish_phase():
         for slot in (4, 5):
             for p in range(3):
-                ring(p, ph, slot, True).wait_recv()
-                if ph == 2:
-                    across(p, slot - 1, False).start()
+                ring(p, slot, True).wait_recv()
+                across(p, slot - 1, False).start()
+
+    def across_wait():
+        for p in range(3):
+            for k in range(5):
+                across(p, k, True).wait_recv()
 
     def rs_copy(step, d, recv):
         if step == 0:
@@ -174,6 +189,15 @@
             ref = wslab.at[((y + (2 if recv else 4 - d)) % 4) * 2 + lo, half]
         return remote(ref, ref, wrs.at[which, slot], wrr.at[which, slot], near(1, d))
 
+    def w1_wait():
+        @pl.when(stays)
+        def _():
+            w1_local().wait()
+
+        @pl.when(jnp.logical_not(stays))
+        def _():
+            w1(True).wait_recv()
+
     def wring_start(which):
         for slot in range(4):
             wring(which, slot, False).start()
@@ -187,55 +211,56 @@
         for slot in range(2, 6):
             wring(which, slot, True).wait_recv()
 
-    def cring(u, slot, recv):
-        h, half = u % 3, u // 3
+    def cring(v, slot, recv):
         d = 1 if slot % 2 == 0 else 3
         if slot < 2:
-            ref = cbuf.at[half, h, (z + (4 - d if recv else 0)) % 4, c]
+            ref = cbuf.at[v, (z + (4 - d if recv else 0)) % 4, c]
         else:
-            ref = cbuf.at[half, h, (z + (2 if recv else 4 - d)) % 4, c, pl.ds((slot - 2) * 256, 256)]
-        return remote(ref, ref, css.at[u, slot], crs.at[u, slot], near(2, d))
-
-    def cacross(u, k, recv):
-        h, half = u % 3, u // 3
+            ref = cbuf.at[v, (z + (2 if recv else 4 - d)) % 4, c, pl.ds(0, 3), pl.ds((slot - 2) * 64, 64)]
+        return remote(ref, ref, css.at[v, slot], crs.at[v, slot], near(2, d))
+
+    def cacross(v, k, recv):
         core = 1 - c if recv else c
         if k < 3:
-            ref = cbuf.at[half, h, (z + (0, 3, 1)[k]) % 4, core]
+            ref = cbuf.at[v, (z + (0, 3, 1)[k]) % 4, core]
         else:
-            ref = cbuf.at[half, h, (z + 2) % 4, core, pl.ds((k - 3) * 256, 256)]
-        return remote(ref, ref, dss.at[u, k], drs.at[u, k], partner)
-
-    def ctx_start(u):
-        cring(u, 0, False).start()
-        cring(u, 1, False).start()
-        cacross(u, 0, False).start()
-
-    def ctx_forward(u):
+            ref = cbuf.at[v, (z + 2) % 4, core, pl.ds(0, 3), pl.ds((k - 3) * 64, 64)]
+        return remote(ref, ref, dss.at[v, k], drs.at[v, k], partner)
+
+    def ctx_start(v):
+        cring(v, 0, False).start()
+        cring(v, 1, False).start()
+        cacross(v, 0, False).start()
+
+    def ctx_forward(v):
         for slot in (0, 1):
-            cring(u, slot, True).wait_recv()
-            cring(u, slot + 2, False).start()
-            cacross(u, 1 + slot, False).start()
-
-    def ctx_finish(u):
+            cring(v, slot, True).wait_recv()
+            cring(v, slot + 2, False).start()
+            cacross(v, 1 + slot, False).start()
+
+    def ctx_finish(v):
         for slot in (2, 3):
-            cring(u, slot, True).wait_recv()
-            cacross(u, 1 + slot, False).start()
-
-    def ctx_ready(u):
+            cring(v, slot, True).wait_recv()
+            cacross(v, 1 + slot, False).start()
+
+    def ctx_ready(v):
         for k in range(5):
-            cacross(u, k, True).wait_recv()
+            cacross(v, k, True).wait_recv()
 
     slab = z * 2 + c
 
-    def owner(half, t):
-        return (t // 4) * 8 + (t % 4) * 2 + half
-
-    def send(half, t):
-        return remote(part.at[half * 8 + t], rbuf.at[x_hi, slab], fss.at[half * 8 + t], frs.at[x_hi, slab],
-                      (row, owner(half, t)))
+    def owner(v, q):
+        return (q // 4) * 8 + (q % 4) * 2 + v // 4
+
+    def sixteen(v):
+        return pl.ds(pl.multiple_of((v % 4) * 16, 16), 16)
+
+    def send(v, q):
+        return remote(part.at[v, pl.ds(q * 16, 16)], rbuf.at[x_hi, slab, sixteen(v)],
+                      fss.at[v, q], frs.at[x_hi, slab], (row, owner(v, q)))
 
     def arrival(hi, t):
-        return remote(part.at[0], rbuf.at[hi, t], fss.at[0], frs.at[hi, t], (row, hi * 8 + t))
+        return remote(rbuf.at[hi, t], rbuf.at[hi, t], fss.at[0, 0], frs.at[hi, t], (row, hi * 8 + t))
 
     p_copy = pltpu.make_async_copy(p_hbm, p2d, osem.at[2])
     p_copy.start()
@@ -265,15 +290,7 @@
             cp.start()
 
         pl.semaphore_wait(barrier, jnp.where(stays, len(peers) + 15, len(peers) + 16))
-        start_phase(0)
-
-        @pl.when(stays)
-        def _():
-            w1_local().start()
-
-        @pl.when(jnp.logical_not(stays))
-        def _():
-            w1(False).start()
+        cast_start(0)
         p_copy.wait()
         own_copies = [
             pltpu.make_async_copy(p2d.at[:, pl.ds(p * 256, 256)], buf.at[p, x, y, z, c], osem.at[3 + p])
@@ -301,13 +318,16 @@
             if t < 4:
                 lhs[ROW_R + 16 * t:ROW_R + 16 * t + 16, 0:3072] = (table * gain_lo).astype(BF16)
         bias_c = (bias - jnp.mean(bias, axis=1, keepdims=True)) * gain
-        tail_rows = lax.broadcasted_iota(jnp.int32, (32, 6144), 0)
-        lhs[ROW_BIAS:ROW_BIAS + 32, :] = jnp.where(
+        tail_rows = lax.broadcasted_iota(jnp.int32, (48, 6144), 0)
+        lhs[ROW_BIAS:ROW_BIAS + 48, :] = jnp.where(
             tail_rows == 0, bias_c, jnp.where(tail_rows == 1, gain, 0.0)).astype(BF16)
 
         for cp in wp_copies:
             cp.wait()
-        forward_phase(0)
+        for cp in own_copies:
+            cp.wait()
+        cast_wait(0)
+        cast_start(1)
 
         def own_table(n):
             sav, cav = sa[pl.ds(n, 1), :], ca[pl.ds(n, 1), :]
@@ -327,11 +347,6 @@
             e = e.reshape(64, 512)
             emb[:, lo:lo + 512] = e
             total = total + jnp.sum(e, axis=1, keepdims=True)
-        for cp in own_copies:
-            cp.wait()
-        direct_phase(0)
-        finish_phase(0)
-        start_phase(1)
         mean = total * (1.0 / 6144)
         square = jnp.zeros((64, 1), F32)
         for n in range(12):
@@ -350,44 +365,47 @@
             lhs[pl.ds(pl.multiple_of(i * 48, 48), 48), :] = w.astype(BF16)
             return carry
 
-        lax.fori_loop(0, 8, center, 0)
-        forward_phase(1)
+        lax.fori_loop(0, 5, center, 0)
         rs_own_copy.wait()
         rs_wait(0)
         rs_step(1)
-        lax.fori_loop(8, 16, center, 0)
-        direct_phase(1)
-        finish_phase(1)
-        start_phase(2)
+        lax.fori_loop(5, 11, center, 0)
+        rs_wait(1)
+        rs_step(2)
+        cast_wait(1)
+        start_phase()
         for p in range(3):
             across(p, 0, False).start()
-        rs_wait(1)
-        rs_step(2)
+        lax.fori_loop(11, 16, center, 0)
         for cp in wq_copies:
             cp.wait()
 
         def product(it, carry):
-            pair = it // 2
-            rows = pl.ds(pl.multiple_of((it % 2) * 496, 496), 496)
+            pair = it // 3
+            rows = pl.ds(pl.multiple_of((it % 3) * LHS_TILE, LHS_TILE), LHS_TILE)
             second = jnp.minimum(2 * pair + 1, 8)
             w = jnp.concatenate([wq[2 * pair], wq[second]], axis=1)
             res[pair, rows, :] = jnp.dot(lhs[rows, :], w, preferred_element_type=F32)
 
-            @pl.when(it == 2)
+            @pl.when(it == 0)
             def _():
                 rs_wait(2)
                 rs_step(3)
 
             @pl.when(it == 5)
             def _():
-                forward_phase(2)
-
-            @pl.when(it == 8)
-            def _():
-                direct_phase(2)
+                forward_phase()
+
+            @pl.when(it == 10)
+            def _():
+                direct_phase()
+
+            @pl.when(it == 14)
+            def _():
+                finish_phase()
             return carry
 
-        lax.fori_loop(0, 10, product, 0)
+        lax.fori_loop(0, 15, product, 0)
 
         mus = mu[...]
         for b in range(9):
@@ -404,21 +422,17 @@
             wres[:, lanes] = w.astype(BF16)
             rpos[:, lanes] = rp
             cpos[:, lanes] = cp
-        finish_phase(2)
         rs_wait(3)
+
+        across_wait()
 
         @pl.when(stays)
         def _():
-            w1_local().wait()
+            w1_local().start()
 
         @pl.when(jnp.logical_not(stays))
         def _():
-            w1(True).wait_recv()
-        wx(False).start()
-        wring_start(0)
-        for p in range(3):
-            for k in range(5):
-                across(p, k, True).wait_recv()
+            w1(False).start()
 
     pl.run_scoped(
         prepare,
@@ -429,11 +443,19 @@
         pltpu.VMEM((128, 128), F32),
     )
 
-    def attend(tiles, kall, vall, qall):
+    def attend(tiles, feats, feats2, kall, vall, qall):
         def tile_copies(n, slot):
             return [
                 pltpu.make_async_copy(buf.at[p, n // 4, n % 4], tiles.at[slot, p], tsem.at[slot, p])
                 for p in range(3)]
+
+        def tile_start(n, slot):
+            for cp in tile_copies(n, slot):
+                cp.start()
+
+        def tile_wait(n, slot):
+            for cp in tile_copies(n, slot):
+                cp.wait()
 
         scale = math.log2(math.e) / math.sqrt(128.0)
 
@@ -445,133 +467,164 @@
             rp = rpos[pl.ds(pl.multiple_of(r * 8, 8), 8), first:first + width]
             cp = cpos[pl.ds(pl.multiple_of((cx // 2) * 64, 64), 64), first:first + width]
             yv = yv + rp.reshape(1, 8, 1, width) + cp.reshape(8, 1, 8, width)
-            rst = jnp.concatenate([rsbuf[cx, cy].reshape(8, 128), jnp.zeros((120, 128), F32)], axis=0).T
-            rcol = jnp.concatenate([rst[0:64, q:q + 1] for q in range(8)], axis=0)
-            return yv.reshape(512, width), rcol
+            return yv.reshape(512, width)
+
+        def rstd_of(n):
+            rows = rsbuf[n // 4, n % 4].reshape(8, 128)
+            rst = jnp.concatenate([rows, jnp.zeros((120, 128), F32)], axis=0).T
+            return jnp.concatenate([rst[0:64, q:q + 1] for q in range(8)], axis=0)
 
         def normed(yh, rcol, gain):
             var = jnp.mean(yh * yh, axis=1, keepdims=True)
             return yh * (rcol * lax.rsqrt(rcol * rcol * var + NORM_EPS)) * gain
 
-        for cp in tile_copies(0, 0):
-            cp.start()
-
-        def fill(n, carry):
-            slot = n % 2
-
-            @pl.when(n + 1 < 16)
-            def _():
-                for cp in tile_copies(n + 1, 1 - slot):
-                    cp.start()
-            for cp in tile_copies(n, slot):
-                cp.wait()
-            yv, rcol = project(n, slot, 384, 768)
+        def store_kv(n, ref):
+            rcol = rstd_of(n)
             at = pl.ds(pl.multiple_of(n * 512, 512), 512)
             for h in range(3):
-                kall[h, at, :] = normed(yv[:, h * 128:h * 128 + 128], rcol, qk_gain[h, 1:2, :]).astype(BF16)
-                vall[h, at, :] = (yv[:, 384 + h * 128:512 + h * 128] * rcol).astype(BF16)
-
+                yk = ref[:, h * 128:h * 128 + 128]
+                kall[h, at, :] = normed(yk, rcol, qk_gain[h, 1:2, :]).astype(BF16)
+                vall[h, at, :] = (ref[:, 384 + h * 128:512 + h * 128] * rcol).astype(BF16)
+
+        def store_q(n, slot):
             @pl.when((n % 4 == y) & ((n // 4) % 2 == x_lo))
             def _():
-                yq, rq = project(n, slot, 0, 384)
+                yq, rq = project(n, slot, 0, 384), rstd_of(n)
                 for h in range(3):
                     qh = normed(yq[:, h * 128:h * 128 + 128], rq, qk_gain[h, 0:1, :] * scale).reshape(8, 8, 8, 128)
-                    for i in range(8):
-                        dst = (n // 8) * 512 + i * 64
-                        qall[h, pl.ds(pl.multiple_of(dst, 64), 64), :] = qh[:, i].reshape(64, 128).astype(BF16)
-
-            @pl.when(n == 12)
-            def _():
-                wring_forward(0)
+                    for t in range(4):
+                        for i in range(8):
+                            dst = (n // 8) * 512 + t * 128 + i * 16
+                            qall[h, pl.ds(pl.multiple_of(dst, 16), 16), :] = (
+                                qh[2 * t:2 * t + 2, i].reshape(16, 128).astype(BF16))
+
+        tile_start(0, 0)
+        tile_start(1, 1)
+        tile_wait(0, 0)
+        store_q(0, 0)
+        feats[...] = project(0, 0, 384, 768)
+        tile_start(2, 0)
+
+        def fill(m, carry):
+            n = 2 * m
+            tile_wait(n + 1, 1)
+            store_q(n + 1, 1)
+            feats2[...] = project(n + 1, 1, 384, 768)
+            store_kv(n, feats)
+
+            @pl.when(m < 7)
+            def _():
+                tile_start(n + 3, 1)
+                tile_wait(n + 2, 0)
+                store_q(n + 2, 0)
+            nxt = jnp.minimum(n + 2, 14)
+            feats[...] = project(nxt, 0, 384, 768)
+            store_kv(n + 1, feats2)
+
+            @pl.when(m < 6)
+            def _():
+                tile_start(n + 4, 0)
+
+            @pl.when(m == 5)
+            def _():
+                w1_wait()
+                wx(False).start()
+                wring_start(0)
+            return carry
+
+        lax.fori_loop(0, 8, fill, 0)
+
+        ones = jnp.ones((8192, 128), BF16)
+
+        def project_out(v):
+            a = jnp.concatenate([cbuf[v, t // 2, t % 2, h] for h in range(3) for t in range(8)], axis=1)
+            w = []
+            for h in range(3):
+                for t in range(8):
+                    if h == 0:
+                        w.append(wslab[t, 0, 0:128, :])
+                    elif h == 2:
+                        w.append(wslab[t, 1, 64:192, :])
+                    else:
+                        w.append(wslab[t, 0, 128:192, :])
+                        w.append(wslab[t, 1, 0:64, :])
+            rows = jnp.dot(a, jnp.concatenate(w, axis=0), preferred_element_type=F32).astype(BF16)
+            part[v] = rows
+            for q in range(8):
+                @pl.when(owner(v, q) == col)
+                def _():
+                    rbuf[x_hi, slab, sixteen(v), :] = rows[q * 16:q * 16 + 16, :]
+
+        def ship(v):
+            for q in range(8):
+                @pl.when(owner(v, q) != col)
+                def _():
+                    send(v, q).start()
+
+        def unit(v, carry):
+            at = pl.ds(pl.multiple_of(v * QT, QT), QT)
+            scores = [
+                lax.dot_general(qall[h, at, :], kall[h], (((1,), (1,)), ((), ())), preferred_element_type=F32)
+                for h in range(3)]
+            for h in range(3):
+                p = jnp.exp2(scores[h] - jnp.max(scores[h], axis=1, keepdims=True)).astype(BF16)
+                a = jnp.dot(p, jnp.concatenate([vall[h], ones], axis=1), preferred_element_type=F32)
+                cbuf[v, z, c, h] = (a[:, :128] / a[:, 128:]).astype(BF16)
+
+            @pl.when(v >= 2)
+            def _():
+                ctx_finish(v - 2)
+
+            @pl.when(v >= 1)
+            def _():
+                ctx_forward(v - 1)
+            ctx_start(v)
+
+            @pl.when(v == 1)
+            def _():
                 wx(True).wait_recv()
                 wring_start(1)
+                wring_forward(0)
+
+            @pl.when(v == 5)
+            def _():
+                wring_forward(1)
             return carry
 
-        lax.fori_loop(0, 16, fill, 0)
-
-        ones = jnp.ones((8192, 128), BF16)
-
-        def partial_rows(half, i, heads):
-            rows = pl.ds(pl.multiple_of(i * 256, 256), 256)
-            total = None
-            for h in heads:
-                a = jnp.concatenate([cbuf[half, h, t // 2, t % 2, rows, :] for t in range(8)], axis=1)
-                w = jnp.concatenate(
-                    [wslab[t, h * 128 // 192, (h * 128) % 192:(h * 128) % 192 + 128, :] if h != 1 else
-                     jnp.concatenate([wslab[t, 0, 128:192, :], wslab[t, 1, 0:64, :]], axis=0) for t in range(8)], axis=0)
-                d = jnp.dot(a, w, preferred_element_type=F32)
-                total = d if total is None else total + d
-            return total
-
-        def ship(half, i, rows):
-            for q in range(4):
-                t = i * 4 + q
-                part[half * 8 + t] = rows[q * 64:q * 64 + 64, :]
-
-                @pl.when(owner(half, t) == col)
-                def _():
-                    rbuf[x_hi, slab] = rows[q * 64:q * 64 + 64, :]
-
-                @pl.when(owner(half, t) != col)
-                def _():
-                    send(half, t).start()
-
-        def unit(u, carry):
-            h, half = u % 3, u // 3
-            k = kall[h]
-            va = jnp.concatenate([vall[h], ones], axis=1)
-            scores = [
-                lax.dot_general(
-                    qall[h, pl.ds(pl.multiple_of(half * 512 + t * QT, QT), QT), :], k,
-                    (((1,), (1,)), ((), ())), preferred_element_type=F32)
-                for t in range(CHAINS)]
-            for t in range(CHAINS):
-                p = jnp.exp2(scores[t] - jnp.max(scores[t], axis=1, keepdims=True)).astype(BF16)
-                a = jnp.dot(p, va, preferred_element_type=F32)
-                cbuf[half, h, z, c, t * QT:t * QT + QT, :] = (a[:, :128] / a[:, 128:]).astype(BF16)
-
-            @pl.when(u >= 2)
-            def _():
-                ctx_finish(u - 2)
-
-            @pl.when(u >= 1)
-            def _():
-                ctx_forward(u - 1)
-            ctx_start(u)
-
-            @pl.when(u == 1)
-            def _():
-                wring_forward(1)
-
-            @pl.when(u == 4)
-            def _():
-                wring_finish(0)
-                wring_finish(1)
-                for v in range(3):
-                    ctx_ready(v)
-
-                def tile(i, carry2):
-                    ship(0, i, partial_rows(0, i, (0, 1, 2)).astype(BF16))
-                    return carry2
-                lax.fori_loop(0, 2, tile, 0)
+        lax.fori_loop(0, 8, unit, 0)
+        wring_finish(0)
+        wring_finish(1)
+
+        def tail_unit(v, carry):
+            @pl.when(v == 4)
+            def _():
+                ctx_forward(7)
+                ctx_finish(6)
+
+            @pl.when(v == 6)
+            def _():
+                ctx_finish(7)
+            ctx_ready(v)
+            project_out(v)
+
+            @pl.when(v < 3)
+            def _():
+                ship(v)
+
+            @pl.when(v == 6)
+            def _():
+                for t in range(3, 7):
+                    ship(t)
             return carry
 
-        lax.fori_loop(0, 6, unit, 0)
-        ctx_finish(4)
-        for v in (3, 4):
-            ctx_ready(v)
-        ctx_forward(5)
-        ctx_finish(5)
-        ctx_ready(5)
-
-        def last_tile(i, carry):
-            ship(1, i, partial_rows(1, i, (0, 1, 2)).astype(BF16))
-            return carry
-        lax.fori_loop(0, 2, last_tile, 0)
+        lax.fori_loop(0, 8, tail_unit, 0)
+        ship(7)
 
     pl.run_scoped(
         attend,
         pltpu.VMEM((2, 3, 4, 2, 64, 256), BF16),
+        pltpu.VMEM((512, 768), F32),
+        pltpu.VMEM((512, 768), F32),
         pltpu.VMEM((3, 8192, 128), BF16),
         pltpu.VMEM((3, 8192, 128), BF16),
         pltpu.VMEM((3, 1024, 128), BF16),
@@ -585,9 +638,11 @@
         out[:, t * 768:t * 768 + 768] = (rbuf[0, t].astype(F32) + rbuf[1, t].astype(F32)).astype(BF16)
 
     for p in range(3):
-        for ph in range(3):
-            for slot in range(6):
-                ring(p, ph, slot, False).wait_send()
+        for ph in range(2):
+            for d in (1, 2, 3):
+                cast(p, ph, d, False).wait_send()
+        for slot in range(6):
+            ring(p, slot, False).wait_send()
         for k in range(5):
             across(p, k, False).wait_send()
     for step in range(4):
@@ -602,16 +657,18 @@
         for slot in range(6):
             wring(which, slot, False).wait_send()
 
-    for u in range(6):
+    def left(v, carry):
         for slot in range(4):
-            cring(u, slot, False).wait_send()
+            cring(v, slot, False).wait_send()
         for k in range(5):
-            cacross(u, k, False).wait_send()
-    for half in range(2):
-        for t in range(8):
-            @pl.when(owner(half, t) != col)
-            def _():
-                send(half, t).wait_send()
+            cacross(v, k, False).wait_send()
+        for q in range(8):
+            @pl.when(owner(v, q) != col)
+            def _():
+                send(v, q).wait_send()
+        return carry
+
+    lax.fori_loop(0, 8, left, 0)
 
 
 def fused(bg, qk_gain, patches, w_patch, w_qkv, w_out):
@@ -634,14 +691,15 @@
             pltpu.VMEM((768, 1152), BF16),
             pltpu.VMEM((64, 1152), F32),
             pltpu.VMEM((128, 1152), F32),
-            pltpu.VMEM((2, 3, 4, 2, 512, 128), BF16),
+            pltpu.VMEM((8, 4, 2, 3, 128, 128), BF16),
             pltpu.VMEM((8, 2, 192, 768), BF16),
-            pltpu.VMEM((16, 64, 768), BF16),
+            pltpu.VMEM((8, 128, 768), BF16),
             pltpu.VMEM((2, 8, 64, 768), BF16),
-            dma((3, 3, 6)), dma((3, 3, 6)), dma((3, 5)), dma((3, 5)),
+            dma((3, 6)), dma((3, 6)), dma((3, 5)), dma((3, 5)),
             dma((4, 4)), dma((4, 4)), dma((4,)), dma((9,)), dma((6,)),
             dma, dma, dma, dma, dma((2, 6)), dma((2, 6)),
-            dma((6, 4)), dma((6, 4)), dma((6, 5)), dma((6, 5)), dma((16,)), dma((2, 8)), dma((2, 3)),
+            dma((8, 4)), dma((8, 4)), dma((8, 5)), dma((8, 5)), dma((8, 8)), dma((2, 8)), dma((2, 3)),
+            dma((3, 2, 4)), dma((3, 2, 4)),
         ],
         compiler_params=pltpu.CompilerParams(collective_id=0, has_side_effects=True, vmem_limit_bytes=VMEM_LIMIT),
         name="fused",

time: 182 us -> 157 us (0.86)
  Pallas kernels: 175 us -> 151 us
    pallas_call x1, Pallas kernels: 175 us -> 151 us  [fused(): pl.pallas_call(fused_kernel, out_shape=(jax.ShapeDtypeStruct((64, 6144),...]
where the time goes in v3:
time: 157 us; the launch traced here: 155 us
  Pallas kernels  151 us (96%)
  local copies, waits for them, and re-layouts  3.51 us (2%)
    pallas_call x1, Pallas kernels, fused(): pl.pallas_call(fused_kernel, out_shape=(jax.ShapeDtypeStruct((64, 6144),...  151 us

profile of v3, /device:TPU:25, one launch (start us, length us, event | category | flops | bytes accessed | tf_op | source)
XLA Modules:
  0.0 155.3 jit_solution(12625197414942187223)
XLA Ops:
  0.0 0.7 stack.9
  0.7 0.7 stack.10
  1.5 0.7 maximum_convert_fusion.bg
  2.1 151.1 %fused.1 = (bf16[64,6144]{1,0:T(8,128)(2,1)}, bf16[3,4,4,4,2,64,256]{6,5,4,3,2,1,0:T(8,128)(2,1)}) custom-call(f32[2,6144]{1,0:T(2,128)} %maximum_convert_fusion.bg, f32[3,2,128]{2,1,0:T(2,128)} %bitcast.7, f32[16,1536]{1,0:T(8,128)} %constant.8.clone.sa, f32[16,1536]{1,0:T(8,128)} %constant.9.clone.ca, f32[8,1536]{1,0:T(8,128)} %constant.10.clone.sb, ...), custom_call_target="tpu_custom_call" | custom-call | tf_op jit(solution)/shard_map/fused/pallas_call | solution.py:679
  153.2 2.1 %copy.13 = bf16[64,6144]{1,0:T(8,128)(2,1)} copy(bf16[64,6144]{1,0:T(8,128)(2,1)} %get-tuple-element.6) | data formatting | bytes 1572864

commit v4 on v3

--- a/solution.py
+++ b/solution.py
@@ -256,7 +256,7 @@
         return pl.ds(pl.multiple_of((v % 4) * 16, 16), 16)
 
     def send(v, q):
-        return remote(part.at[v, pl.ds(q * 16, 16)], rbuf.at[x_hi, slab, sixteen(v)],
+        return remote(part.at[v, pl.ds(pl.multiple_of(q * 16, 16), 16)], rbuf.at[x_hi, slab, sixteen(v)],
                       fss.at[v, q], frs.at[x_hi, slab], (row, owner(v, q)))
 
     def arrival(hi, t):
@@ -403,6 +403,14 @@
             @pl.when(it == 14)
             def _():
                 finish_phase()
+
+                @pl.when(stays)
+                def _():
+                    w1_local().start()
+
+                @pl.when(jnp.logical_not(stays))
+                def _():
+                    w1(False).start()
             return carry
 
         lax.fori_loop(0, 15, product, 0)
@@ -426,14 +434,6 @@
 
         across_wait()
 
-        @pl.when(stays)
-        def _():
-            w1_local().start()
-
-        @pl.when(jnp.logical_not(stays))
-        def _():
-            w1(False).start()
-
     pl.run_scoped(
         prepare,
         pltpu.VMEM((LHS_ROWS, 6144), BF16),
@@ -443,7 +443,7 @@
         pltpu.VMEM((128, 128), F32),
     )
 
-    def attend(tiles, feats, feats2, kall, vall, qall):
+    def attend(tiles, feats, feats2, rwide, kall, vall, qall):
         def tile_copies(n, slot):
             return [
                 pltpu.make_async_copy(buf.at[p, n // 4, n % 4], tiles.at[slot, p], tsem.at[slot, p])
@@ -478,13 +478,27 @@
             var = jnp.mean(yh * yh, axis=1, keepdims=True)
             return yh * (rcol * lax.rsqrt(rcol * rcol * var + NORM_EPS)) * gain
 
-        def store_kv(n, ref):
-            rcol = rstd_of(n)
-            at = pl.ds(pl.multiple_of(n * 512, 512), 512)
-            for h in range(3):
-                yk = ref[:, h * 128:h * 128 + 128]
-                kall[h, at, :] = normed(yk, rcol, qk_gain[h, 1:2, :]).astype(BF16)
-                vall[h, at, :] = (ref[:, 384 + h * 128:512 + h * 128] * rcol).astype(BF16)
+        def both(n, ref, nxt, slot, dest):
+            rwide[...] = jnp.broadcast_to(rstd_of(n), (512, 128))
+            cx, cy = nxt // 4, nxt % 4
+            r = cy * 2 + cx % 2
+            rp = rpos[pl.ds(pl.multiple_of(r * 8, 8), 8), 384:1152].reshape(1, 8, 1, 768)
+
+            def rows(t, carry):
+                here = pl.ds(pl.multiple_of(t * 256, 256), 256)
+                p = jnp.concatenate([tiles[slot, q, pl.ds(t * 2, 2)].reshape(256, 256) for q in range(3)], axis=1)
+                yv = jnp.dot(p, wres[:, 384:1152], preferred_element_type=F32).reshape(4, 8, 8, 768)
+                cp = cpos[pl.ds(pl.multiple_of((cx // 2) * 64 + t * 32, 32), 32), 384:1152]
+                dest[here, :] = (yv + rp + cp.reshape(4, 1, 8, 768)).reshape(256, 768)
+                at = pl.ds(pl.multiple_of(n * 512 + t * 256, 256), 256)
+                rs = rwide[here, :]
+                for h in range(3):
+                    yk = ref[here, h * 128:h * 128 + 128]
+                    kall[h, at, :] = normed(yk, rs, qk_gain[h, 1:2, :]).astype(BF16)
+                    vall[h, at, :] = (ref[here, 384 + h * 128:512 + h * 128] * rs).astype(BF16)
+                return carry
+
+            lax.fori_loop(0, 2, rows, 0)
 
         def store_q(n, slot):
             @pl.when((n % 4 == y) & ((n // 4) % 2 == x_lo))
@@ -509,8 +523,7 @@
             n = 2 * m
             tile_wait(n + 1, 1)
             store_q(n + 1, 1)
-            feats2[...] = project(n + 1, 1, 384, 768)
-            store_kv(n, feats)
+            both(n, feats, n + 1, 1, feats2)
 
             @pl.when(m < 7)
             def _():
@@ -518,8 +531,7 @@
                 tile_wait(n + 2, 0)
                 store_q(n + 2, 0)
             nxt = jnp.minimum(n + 2, 14)
-            feats[...] = project(nxt, 0, 384, 768)
-            store_kv(n + 1, feats2)
+            both(n + 1, feats2, nxt, 0, feats)
 
             @pl.when(m < 6)
             def _():
@@ -556,7 +568,9 @@
                     rbuf[x_hi, slab, sixteen(v), :] = rows[q * 16:q * 16 + 16, :]
 
         def ship(v):
-            for q in range(8):
+            for k in range(8):
+                q = (x_hi + k // 4) % 2 * 4 + (z + k) % 4
+
                 @pl.when(owner(v, q) != col)
                 def _():
                     send(v, q).start()
@@ -596,25 +610,30 @@
         wring_finish(1)
 
         def tail_unit(v, carry):
-            @pl.when(v == 4)
+            @pl.when(v == 2)
+            def _():
+                ctx_finish(6)
+
+            @pl.when(v == 3)
             def _():
                 ctx_forward(7)
-                ctx_finish(6)
+                ship(2)
+
+            @pl.when(v == 5)
+            def _():
+                ship(3)
 
             @pl.when(v == 6)
             def _():
                 ctx_finish(7)
+                ship(4)
+                ship(5)
             ctx_ready(v)
             project_out(v)
 
-            @pl.when(v < 3)
+            @pl.when((v < 2) | (v == 6))
             def _():
                 ship(v)
-
-            @pl.when(v == 6)
-            def _():
-                for t in range(3, 7):
-                    ship(t)
             return carry
 
         lax.fori_loop(0, 8, tail_unit, 0)
@@ -625,6 +644,7 @@
         pltpu.VMEM((2, 3, 4, 2, 64, 256), BF16),
         pltpu.VMEM((512, 768), F32),
         pltpu.VMEM((512, 768), F32),
+        pltpu.VMEM((512, 128), F32),
         pltpu.VMEM((3, 8192, 128), BF16),
         pltpu.VMEM((3, 8192, 128), BF16),
         pltpu.VMEM((3, 1024, 128), BF16),

time: 157 us -> 150 us (0.955)
  Pallas kernels: 151 us -> 145 us
    pallas_call x1, Pallas kernels: 151 us -> 145 us  [fused(): pl.pallas_call(fused_kernel, out_shape=(jax.ShapeDtypeStruct((64, 6144),...]
where the time goes in v4:
time: 150 us; the launch traced here: 149 us
  Pallas kernels  145 us (97%)
  local copies, waits for them, and re-layouts  3.51 us (2%)
    pallas_call x1, Pallas kernels, fused(): pl.pallas_call(fused_kernel, out_shape=(jax.ShapeDtypeStruct((64, 6144),...  145 us

profile of v4, /device:TPU:25, one launch (start us, length us, event | category | flops | bytes accessed | tf_op | source)
XLA Modules:
  0.0 149.4 jit_solution(15708925121603285957)
XLA Ops:
  0.0 0.7 stack.9
  0.7 0.7 stack.10
  1.5 0.7 maximum_convert_fusion.bg
  2.1 145.2 %fused.1 = (bf16[64,6144]{1,0:T(8,128)(2,1)}, bf16[3,4,4,4,2,64,256]{6,5,4,3,2,1,0:T(8,128)(2,1)}) custom-call(f32[2,6144]{1,0:T(2,128)} %maximum_convert_fusion.bg, f32[3,2,128]{2,1,0:T(2,128)} %bitcast.7, f32[16,1536]{1,0:T(8,128)} %constant.8.clone.sa, f32[16,1536]{1,0:T(8,128)} %constant.9.clone.ca, f32[8,1536]{1,0:T(8,128)} %constant.10.clone.sb, ...), custom_call_target="tpu_custom_call" | custom-call | tf_op jit(solution)/shard_map/fused/pallas_call | solution.py:699
  147.4 2.1 %copy.13 = bf16[64,6144]{1,0:T(8,128)(2,1)} copy(bf16[64,6144]{1,0:T(8,128)(2,1)} %get-tuple-element.6) | data formatting | bytes 1572864
